TPU v7x, 256 devices: a whole 4x4x8 slice. The times are simulated.
256 devices in a mesh: bvec: 4 (over x), row: 16 (over z, core), col: 4 (over y).
Axes of the slice: x: 4, y: 4, z: 8, core: 2. Of those that a mesh axis runs over, the one named last changes fastest.
Arguments:
- m_matrices: float32 [4, 2, 2048, 2048], P('bvec', None, 'row', 'col'), may hold values from -2 to 2, as said below
- bvec_index: int32 [4], replicated, may hold values from 0 to 5
- weight_table: float32 [6], replicated, may hold values from 0.25 to 2
- grad_prev: float32 [2048, 2048], P('row', 'col'), may hold values from -4 to 4, as said below
- dir_prev: float32 [2048, 2048], P('row', 'col'), may hold values from -4 to 4, as said below
Outputs:
- spread: float32 [], replicated
- trial_spread: float32 [], replicated
- gradient: float32 [2048, 2048], P('row', 'col')
- direction: float32 [2048, 2048], P('row', 'col')
- trial_diag: float32 [4, 2, 2048], replicated
Inputs may be any that keep to these rules, and one draw needn't show every extreme that they name: Each matrix m_matrices[b, p] is symmetric. grad_prev is antisymmetric. dir_prev is antisymmetric.
All inputs are finite; a program needn't handle non-finite values.
Results may differ from a plain program's by a relative error of at most 0.0003.
Values sent between devices are 32-bit elements; how exact they have to be, the bound alone decides.
A program may use at most 64 MiB of HBM per device.

v0:
```python
import jax
import jax.numpy as jnp
from jax import lax
from jax.sharding import Mesh
from jax.sharding import PartitionSpec as P

TAYLOR = 8
ROW = ("row_0", "row_1")
BVEC_ROW_COL = ("bvec", "row_0", "row_1", "col")


STEP_SCALE = 1.75
HIGHEST = lax.Precision.HIGHEST


def sent_to_all(array, axis):
    copies = jnp.broadcast_to(array, (lax.axis_size(axis), *array.shape))
    return lax.all_to_all(copies, axis, split_axis=0, concat_axis=0, tiled=True)


def of_everyone(array, axis):
    return sent_to_all(array, axis).sum(axis=0)


def in_order(parts, dim):
    lengths = list(parts.shape[1:])
    lengths[dim] *= parts.shape[0]
    return jnp.moveaxis(parts, 0, dim).reshape(lengths)


def gathered_copies(array, axis, dim):
    return in_order(sent_to_all(array, axis), dim)


def over_axes(array, axes):
    for axis in axes:
        array = lax.psum(array, axis)
    return array


def product(left, right):
    return jnp.dot(left, right, precision=HIGHEST, preferred_element_type=jnp.float32)


def lookup_weights(bvec_index, weight_table):
    table_slots = jnp.arange(weight_table.shape[0], dtype=jnp.int32)
    return jnp.sum(
        jnp.where(table_slots[None, :] == bvec_index[:, None], weight_table[None, :], 0.0), axis=1
    )


def shards(m_matrices, bvec_index, weight_table, grad_prev, dir_prev):
    per_group = m_matrices.shape[0]
    local_rows = m_matrices.shape[2]
    local_cols = m_matrices.shape[3]
    matrix_order = local_rows * lax.axis_size(ROW)
    group_index = lax.axis_index("bvec")
    row_start = lax.axis_index(ROW) * local_rows
    col_start = lax.axis_index("col") * local_cols
    weight_all = lookup_weights(bvec_index, weight_table)
    weight_own = lax.dynamic_slice_in_dim(weight_all, group_index * per_group, per_group)
    row_ids = row_start + jnp.arange(local_rows, dtype=jnp.int32)
    col_ids = col_start + jnp.arange(local_cols, dtype=jnp.int32)
    on_diag = (row_ids[:, None] == col_ids[None, :]).astype(jnp.float32)
    own_diag = jnp.sum(m_matrices * on_diag, axis=2)
    share_diag = of_everyone(own_diag, ROW)
    diagonal = gathered_copies(share_diag, "col", 2)
    row_diag = lax.dynamic_slice_in_dim(diagonal, row_start, local_rows, 2)
    spread_own = (
        jnp.sum(weight_own[:, None] * (1.0 - diagonal[:, 0] ** 2 - diagonal[:, 1] ** 2))
        / matrix_order
    )
    leader = (lax.axis_index(ROW) == 0) & (lax.axis_index("col") == 0)
    spread_term = jnp.where(leader, spread_own, 0.0)
    differ = row_diag[:, :, :, None] - share_diag[:, :, None, :]
    weighted = 2.0 * weight_own[:, None, None] * jnp.sum(m_matrices * differ, axis=1)
    grad_part = jnp.sum(weighted, axis=0)
    gradient = of_everyone(grad_part, "bvec")
    counted = jnp.where(group_index == 0, 1.0, 0.0)
    grad_square = counted * jnp.sum(gradient * gradient)
    prev_square = counted * jnp.sum(grad_prev * grad_prev)
    cross_term = counted * jnp.sum(gradient * dir_prev)
    dir_square = counted * jnp.sum(dir_prev * dir_prev)
    totals = (
        over_axes(spread_term, BVEC_ROW_COL),
        over_axes(grad_square, BVEC_ROW_COL),
        over_axes(prev_square, BVEC_ROW_COL),
        over_axes(cross_term, BVEC_ROW_COL),
        over_axes(dir_square, BVEC_ROW_COL),
    )
    spread = totals[0]
    beta_factor = totals[1] / (1.0 + totals[2])
    direction = beta_factor * dir_prev - gradient
    dir_norm = jnp.maximum(
        totals[1] - 2.0 * beta_factor * totals[3] + beta_factor * beta_factor * totals[4], 0.0
    )
    generator = STEP_SCALE * direction / jnp.sqrt(1.0 + dir_norm / matrix_order)
    block_ids = col_start + jnp.arange(local_cols, dtype=jnp.int32)
    eye_block = (row_ids[:, None] == block_ids[None, :]).astype(jnp.float32)
    horner_start = eye_block + generator / TAYLOR
    columns = lax.all_gather(generator, ROW, axis=0, tiled=True)

    def accumulate(section):
        return product(section, columns)

    def horner_step(counter, current):
        folded = accumulate(gathered_copies(current, "col", 1))
        divisor = (TAYLOR - 1 - counter).astype(jnp.float32)
        return eye_block + folded / divisor

    expmap = lax.fori_loop(0, TAYLOR - 1, horner_step, horner_start)
    expmap_cols = lax.all_gather(expmap, ROW, axis=0, tiled=True)
    section = gathered_copies(m_matrices, "col", 3)
    flattened = section.reshape((-1, section.shape[3]))
    rotated = product(flattened, expmap_cols).reshape(
        jnp.zeros(m_matrices.shape, jnp.float32).shape
    )
    trial_part = jnp.sum(expmap[None, None] * rotated, axis=2)
    trial_share = of_everyone(trial_part, ROW)
    trial_group = gathered_copies(trial_share, "col", 2)
    trial_diag = gathered_copies(trial_group, "bvec", 0)
    trial_spread = (
        jnp.sum(weight_all[:, None] * (1.0 - trial_diag[:, 0] ** 2 - trial_diag[:, 1] ** 2))
        / matrix_order
    )
    return (spread, trial_spread, gradient, direction, trial_diag)


def solution(mesh):
    torus = Mesh(
        mesh.devices.reshape(mesh.shape["bvec"], 8, 2, mesh.shape["col"]),
        ("bvec", "row_0", "row_1", "col"),
    )
    placed = (P("bvec", None, ROW, "col"), P(), P(), P(ROW, "col"), P(ROW, "col"))
    return jax.shard_map(
        shards,
        mesh=torus,
        in_specs=placed,
        out_specs=(P(), P(), P(ROW, "col"), P(ROW, "col"), P()),
        check_vma=False,
    )
```

profile of v0, /device:TPU:1, one launch (start us, length us, event | category | flops | bytes accessed | tf_op | source)
XLA Modules:
  0.0 379.1 jit_solution(14576557958084498844)
XLA Ops:
  8.5 17.5 %all_to_all.46 = f32[16,1,2,512]{3,2,1,0:T(2,128)S(1)} all-to-all(f32[16,1,2,512]{3,2,1,0:T(2,128)S(1)} %broadcast_in_dim.56), channel_id=1, replica_groups=mesh['bvec'=4,'row_0'=8,'row_1'=2,'col'=4] {'row_0','row_1'}, dimensions={0} | all-to-all | bytes 131072 | tf_op jit(solution)/shard_map/all_to_all | solution.py:18
  26.7 4.2 %all-to-all-start.2 = ((f32[4,1,2,512]{3,2,1,0:T(2,128)}), f32[4,1,2,512]{3,2,1,0:T(2,128)S(1)}, u32[]{:S(2)}, u32[]{:S(2)}) async-start(f32[4,1,2,512]{3,2,1,0:T(2,128)} %broadcast_in_dim.57), calls=%async_computation.2 | async-start | bytes 32768 | tf_op jit(solution)/shard_map/all_to_all | solution.py:18
  37.4 4.0 %all-to-all-start.3 = ((f32[4,128,512]{2,1,0:T(8,128)}), f32[4,128,512]{2,1,0:T(8,128)S(1)}, u32[]{:S(2)}, u32[]{:S(2)}) async-start(f32[4,128,512]{2,1,0:T(8,128)} %broadcast_in_dim.58), calls=%async_computation.3 | async-start | bytes 2097152 | tf_op jit(solution)/shard_map/all_to_all | solution.py:18
  44.7 10.1 %all-to-all-done.3 = f32[4,128,512]{2,1,0:T(8,128)S(1)} async-done(((f32[4,128,512]{2,1,0:T(8,128)}), f32[4,128,512]{2,1,0:T(8,128)S(1)}, u32[]{:S(2)}, u32[]{:S(2)}) %all-to-all-start.3) | async-done | bytes 1048608 | tf_op jit(solution)/shard_map/all_to_all | solution.py:18
  57.6 7.5 %all-reduce.2 = (f32[]{:T(128)}, f32[]{:T(128)}, f32[]{:T(128)}, f32[]{:T(128)}, f32[]{:T(128)}) all-reduce(f32[]{:T(128)S(6)} %select_n.20, f32[]{:T(128)S(6)} %mul.144, f32[]{:T(128)S(6)} %mul.146, f32[]{:T(128)S(6)} %mul.153, f32[]{:T(128)S(6)} %mul.157), channel_id=1, replica_groups=mesh['bvec'=4,'row_0'=8,'row_1'=2,'col'=4] {'bvec'}, use_global_device_ids=true, to_apply=%region_4.5 | all-reduce | flops 5 | bytes 40 | tf_op jit(solution)/shard_map/psum | solution.py:37
  65.0 11.4 %all-reduce = (f32[]{:T(128)}, f32[]{:T(128)}, f32[]{:T(128)}, f32[]{:T(128)}, f32[]{:T(128)}) all-reduce(f32[]{:T(128)} %get-tuple-element.122, f32[]{:T(128)} %get-tuple-element.123, f32[]{:T(128)} %get-tuple-element.124, f32[]{:T(128)} %get-tuple-element.125, ...), channel_id=1, replica_groups=mesh['bvec'=4,'row_0'=8,'row_1'=2,'col'=4] {'row_0'}, use_global_device_ids=true, to_apply=%region_5.6 | all-reduce | flops 5 | bytes 40 | tf_op jit(solution)/shard_map/psum | solution.py:37
  76.5 11.4 %all-reduce.3 = (f32[]{:T(128)}, f32[]{:T(128)}, f32[]{:T(128)}, f32[]{:T(128)}, f32[]{:T(128)}) all-reduce(f32[]{:T(128)} %get-tuple-element.112, f32[]{:T(128)} %get-tuple-element.113, f32[]{:T(128)} %get-tuple-element.114, f32[]{:T(128)} %get-tuple-element.115, ...), channel_id=1, replica_groups=mesh['bvec'=4,'row_0'=8,'row_1'=2,'col'=4] {'row_1'}, use_global_device_ids=true, to_apply=%region_6.7 | all-reduce | flops 5 | bytes 40 | tf_op jit(solution)/shard_map/psum | solution.py:37
  87.9 7.6 %all-reduce.1 = (f32[]{:T(128)}, f32[]{:T(128)}, f32[]{:T(128)}, f32[]{:T(128)}, f32[]{:T(128)}) all-reduce(f32[]{:T(128)} %get-tuple-element.127, f32[]{:T(128)} %get-tuple-element.128, f32[]{:T(128)} %get-tuple-element.129, f32[]{:T(128)} %get-tuple-element.130, ...), channel_id=1, replica_groups=mesh['bvec'=4,'row_0'=8,'row_1'=2,'col'=4] {'col'}, use_global_device_ids=true, to_apply=%region_7.8 | all-reduce | flops 5 | bytes 40 | tf_op jit(solution)/shard_map/psum | solution.py:37
  99.6 38.1 %all-gather.3.cloned.1.call-done = f32[2048,512]{1,0:T(8,128)} async-done(((f32[128,512]{1,0:T(8,128)}), f32[2048,512]{1,0:T(8,128)}) %all-gather.3.cloned.1.call-update) | async-done | bytes 4194320 | tf_op jit(solution)/shard_map/all_gather | solution.py:101
  137.8 150.0 %while.14 = (s32[]{:T(128)}, f32[128,512]{1,0:T(8,128)S(1)}, f32[2048,512]{1,0:T(8,128)}, s32[512]{0:T(512)S(1)}, s32[128]{0:T(128)S(1)}, /*index=5*/s32[]{:T(128)}, s32[]{:T(128)}) while((s32[]{:T(128)}, f32[128,512]{1,0:T(8,128)S(1)}, f32[2048,512]{1,0:T(8,128)}, s32[512]{0:T(512)S(1)}, s32[128]{0:T(128)S(1)}, ...), condition=%wide.region_31.32_spmd.clone, body=%wide.region_30.31_spmd.clone.sunk | while | flops 1610874880 | bytes 10488453 | solution.py:111
  138.9 4.0 %all-to-all-start = ((f32[4,128,512]{1,2,0:T(8,128)}), f32[4,128,512]{1,2,0:T(8,128)S(1)}, u32[]{:S(2)}, u32[]{:S(2)}) async-start(f32[4,128,512]{1,2,0:T(8,128)} %broadcast_in_dim.67), calls=%async_computation | async-start | bytes 2097152 | tf_op jit(solution)/shard_map/while/body/eval_jaxpr/all_to_all | solution.py:18
  142.9 14.6 %all-to-all-done = f32[4,128,512]{1,2,0:T(8,128)S(1)} async-done(((f32[4,128,512]{1,2,0:T(8,128)}), f32[4,128,512]{1,2,0:T(8,128)S(1)}, u32[]{:S(2)}, u32[]{:S(2)}) %all-to-all-start) | async-done | bytes 1048608 | tf_op jit(solution)/shard_map/while/body/eval_jaxpr/all_to_all | solution.py:18
  157.6 4.8 %fusion.18 = f32[128,512]{1,0:T(8,128)S(1)} fusion(f32[128,2048]{0,1:T(8,128)S(1)} %bitcast.36, f32[2048,512]{1,0:T(8,128)} %get-tuple-element.182, s32[512]{0:T(512)S(1)} %get-tuple-element.183, f32[]{:T(128)S(6)} %convert_element_type.28, s32[128]{0:T(128)S(1)} %get-tuple-element.184), kind=kOutput, calls=%fused_computation.2.clone.1 | convolution fusion | flops 1610874880 | bytes 5507588 | tf_op jit(solution)/shard_map/while/body/eval_jaxpr/dot_general | solution.py:42
  163.6 3.5 all-to-all-start
  167.1 13.7 %all-to-all-done = f32[4,128,512]{1,2,0:T(8,128)S(1)} async-done(((f32[4,128,512]{1,2,0:T(8,128)}), f32[4,128,512]{1,2,0:T(8,128)S(1)}, u32[]{:S(2)}, u32[]{:S(2)}) %all-to-all-start) | async-done | bytes 1048608 | tf_op jit(solution)/shard_map/while/body/eval_jaxpr/all_to_all | solution.py:18
  180.8 4.8 %fusion.18 = f32[128,512]{1,0:T(8,128)S(1)} fusion(f32[128,2048]{0,1:T(8,128)S(1)} %bitcast.36, f32[2048,512]{1,0:T(8,128)} %get-tuple-element.182, s32[512]{0:T(512)S(1)} %get-tuple-element.183, f32[]{:T(128)S(6)} %convert_element_type.28, s32[128]{0:T(128)S(1)} %get-tuple-element.184), kind=kOutput, calls=%fused_computation.2.clone.1 | convolution fusion | flops 1610874880 | bytes 5507588 | tf_op jit(solution)/shard_map/while/body/eval_jaxpr/dot_general | solution.py:42
  190.3 12.9 %all-to-all-done = f32[4,128,512]{1,2,0:T(8,128)S(1)} async-done(((f32[4,128,512]{1,2,0:T(8,128)}), f32[4,128,512]{1,2,0:T(8,128)S(1)}, u32[]{:S(2)}, u32[]{:S(2)}) %all-to-all-start) | async-done | bytes 1048608 | tf_op jit(solution)/shard_map/while/body/eval_jaxpr/all_to_all | solution.py:18
  203.2 4.8 %fusion.18 = f32[128,512]{1,0:T(8,128)S(1)} fusion(f32[128,2048]{0,1:T(8,128)S(1)} %bitcast.36, f32[2048,512]{1,0:T(8,128)} %get-tuple-element.182, s32[512]{0:T(512)S(1)} %get-tuple-element.183, f32[]{:T(128)S(6)} %convert_element_type.28, s32[128]{0:T(128)S(1)} %get-tuple-element.184), kind=kOutput, calls=%fused_computation.2.clone.1 | convolution fusion | flops 1610874880 | bytes 5507588 | tf_op jit(solution)/shard_map/while/body/eval_jaxpr/dot_general | solution.py:42
  212.7 11.7 %all-to-all-done = f32[4,128,512]{1,2,0:T(8,128)S(1)} async-done(((f32[4,128,512]{1,2,0:T(8,128)}), f32[4,128,512]{1,2,0:T(8,128)S(1)}, u32[]{:S(2)}, u32[]{:S(2)}) %all-to-all-start) | async-done | bytes 1048608 | tf_op jit(solution)/shard_map/while/body/eval_jaxpr/all_to_all | solution.py:18
  224.4 4.8 %fusion.18 = f32[128,512]{1,0:T(8,128)S(1)} fusion(f32[128,2048]{0,1:T(8,128)S(1)} %bitcast.36, f32[2048,512]{1,0:T(8,128)} %get-tuple-element.182, s32[512]{0:T(512)S(1)} %get-tuple-element.183, f32[]{:T(128)S(6)} %convert_element_type.28, s32[128]{0:T(128)S(1)} %get-tuple-element.184), kind=kOutput, calls=%fused_computation.2.clone.1 | convolution fusion | flops 1610874880 | bytes 5507588 | tf_op jit(solution)/shard_map/while/body/eval_jaxpr/dot_general | solution.py:42
  234.0 10.6 %all-to-all-done = f32[4,128,512]{1,2,0:T(8,128)S(1)} async-done(((f32[4,128,512]{1,2,0:T(8,128)}), f32[4,128,512]{1,2,0:T(8,128)S(1)}, u32[]{:S(2)}, u32[]{:S(2)}) %all-to-all-start) | async-done | bytes 1048608 | tf_op jit(solution)/shard_map/while/body/eval_jaxpr/all_to_all | solution.py:18
  244.5 4.8 %fusion.18 = f32[128,512]{1,0:T(8,128)S(1)} fusion(f32[128,2048]{0,1:T(8,128)S(1)} %bitcast.36, f32[2048,512]{1,0:T(8,128)} %get-tuple-element.182, s32[512]{0:T(512)S(1)} %get-tuple-element.183, f32[]{:T(128)S(6)} %convert_element_type.28, s32[128]{0:T(128)S(1)} %get-tuple-element.184), kind=kOutput, calls=%fused_computation.2.clone.1 | convolution fusion | flops 1610874880 | bytes 5507588 | tf_op jit(solution)/shard_map/while/body/eval_jaxpr/dot_general | solution.py:42
  254.0 9.7 %all-to-all-done = f32[4,128,512]{1,2,0:T(8,128)S(1)} async-done(((f32[4,128,512]{1,2,0:T(8,128)}), f32[4,128,512]{1,2,0:T(8,128)S(1)}, u32[]{:S(2)}, u32[]{:S(2)}) %all-to-all-start) | async-done | bytes 1048608 | tf_op jit(solution)/shard_map/while/body/eval_jaxpr/all_to_all | solution.py:18
  263.7 4.8 %fusion.18 = f32[128,512]{1,0:T(8,128)S(1)} fusion(f32[128,2048]{0,1:T(8,128)S(1)} %bitcast.36, f32[2048,512]{1,0:T(8,128)} %get-tuple-element.182, s32[512]{0:T(512)S(1)} %get-tuple-element.183, f32[]{:T(128)S(6)} %convert_element_type.28, s32[128]{0:T(128)S(1)} %get-tuple-element.184), kind=kOutput, calls=%fused_computation.2.clone.1 | convolution fusion | flops 1610874880 | bytes 5507588 | tf_op jit(solution)/shard_map/while/body/eval_jaxpr/dot_general | solution.py:42
  273.3 9.7 %all-to-all-done = f32[4,128,512]{1,2,0:T(8,128)S(1)} async-done(((f32[4,128,512]{1,2,0:T(8,128)}), f32[4,128,512]{1,2,0:T(8,128)S(1)}, u32[]{:S(2)}, u32[]{:S(2)}) %all-to-all-start) | async-done | bytes 1048608 | tf_op jit(solution)/shard_map/while/body/eval_jaxpr/all_to_all | solution.py:18
  283.0 4.8 %fusion.18 = f32[128,512]{1,0:T(8,128)S(1)} fusion(f32[128,2048]{0,1:T(8,128)S(1)} %bitcast.36, f32[2048,512]{1,0:T(8,128)} %get-tuple-element.182, s32[512]{0:T(512)S(1)} %get-tuple-element.183, f32[]{:T(128)S(6)} %convert_element_type.28, s32[128]{0:T(128)S(1)} %get-tuple-element.184), kind=kOutput, calls=%fused_computation.2.clone.1 | convolution fusion | flops 1610874880 | bytes 5507588 | tf_op jit(solution)/shard_map/while/body/eval_jaxpr/dot_general | solution.py:42
  288.8 20.9 %all_to_all.47 = f32[4,1,2,128,512]{4,3,2,1,0:T(8,128)S(1)} all-to-all(f32[4,1,2,128,512]{4,3,2,1,0:T(8,128)S(1)} %broadcast_in_dim.59), channel_id=1, replica_groups=mesh['bvec'=4,'row_0'=8,'row_1'=2,'col'=4] {'col'}, dimensions={0} | all-to-all | bytes 4194304 | tf_op jit(solution)/shard_map/all_to_all | solution.py:18
  311.9 22.9 %all-gather.5.cloned.1.call-done = f32[2048,512]{1,0:T(8,128)} async-done(((f32[128,512]{1,0:T(8,128)}), f32[2048,512]{1,0:T(8,128)}) %all-gather.5.cloned.1.call-update) | async-done | bytes 4194320 | tf_op jit(solution)/shard_map/all_gather | solution.py:112
  334.8 5.8 %fusion.8 = f32[512,256]{0,1:T(8,128)S(1)} fusion(f32[2048,512]{1,0:T(8,128)} %all-gather.5.cloned.1.call-done, f32[256,2048]{1,0:T(8,128)S(1)} %bitcast.37), kind=kOutput, calls=%fused_computation.31 | convolution fusion | flops 3221225472 | bytes 6815744 | tf_op jit(solution)/shard_map/dot_general | solution.py:42
  340.7 12.0 %all_to_all.48 = f32[16,1,2,512]{3,2,1,0:T(2,128)S(1)} all-to-all(f32[16,1,2,512]{3,2,1,0:T(2,128)S(1)} %broadcast_in_dim.60), channel_id=1, replica_groups=mesh['bvec'=4,'row_0'=8,'row_1'=2,'col'=4] {'row_0','row_1'}, dimensions={0} | all-to-all | bytes 131072 | tf_op jit(solution)/shard_map/all_to_all | solution.py:18
  352.8 8.0 %all_to_all.49 = f32[4,1,2,512]{3,2,1,0:T(2,128)S(1)} all-to-all(f32[4,1,2,512]{3,2,1,0:T(2,128)S(1)} %broadcast_in_dim.61), channel_id=1, replica_groups=mesh['bvec'=4,'row_0'=8,'row_1'=2,'col'=4] {'col'}, dimensions={0} | all-to-all | bytes 32768 | tf_op jit(solution)/shard_map/all_to_all | solution.py:18
  360.8 8.2 %all_to_all.50 = f32[4,1,2,2048]{3,2,1,0:T(2,128)S(1)} all-to-all(f32[4,1,2,2048]{3,2,1,0:T(2,128)S(1)} %broadcast_in_dim.62), channel_id=1, replica_groups=mesh['bvec'=4,'row_0'=8,'row_1'=2,'col'=4] {'bvec'}, dimensions={0} | all-to-all | bytes 131072 | tf_op jit(solution)/shard_map/all_to_all | solution.py:18
  (65 shorter events, 41.9 us)
Async XLA Ops:
  7.2 34.3 %copy-start.5 = (f32[128,512]{1,0:T(8,128)S(1)}, f32[128,512]{1,0:T(8,128)}, u32[]{:S(2)}) copy-start(f32[128,512]{1,0:T(8,128)} %param.10) | copy-start | bytes 786436
  7.2 47.7 %copy-start.4 = (f32[128,512]{1,0:T(8,128)S(1)}, f32[128,512]{1,0:T(8,128)}, u32[]{:S(2)}) copy-start(f32[128,512]{1,0:T(8,128)} %param.11) | copy-start | bytes 786436
  26.7 8.4 %all-to-all-start.2 = ((f32[4,1,2,512]{3,2,1,0:T(2,128)}), f32[4,1,2,512]{3,2,1,0:T(2,128)S(1)}, u32[]{:S(2)}, u32[]{:S(2)}) async-start(f32[4,1,2,512]{3,2,1,0:T(2,128)} %broadcast_in_dim.57), calls=%async_computation.2 | async-start | bytes 32768 | tf_op jit(solution)/shard_map/all_to_all | solution.py:18
  37.4 17.4 %all-to-all-start.3 = ((f32[4,128,512]{2,1,0:T(8,128)}), f32[4,128,512]{2,1,0:T(8,128)S(1)}, u32[]{:S(2)}, u32[]{:S(2)}) async-start(f32[4,128,512]{2,1,0:T(8,128)} %broadcast_in_dim.58), calls=%async_computation.3 | async-start | bytes 2097152 | tf_op jit(solution)/shard_map/all_to_all | solution.py:18
  41.4 96.3 %all-gather.3.cloned.1.call-start = ((), (), s32[]{:S(2)}) async-start(), calls=%async_computation.8 | async-start | bytes 4456448 | tf_op jit(solution)/shard_map/all_gather | solution.py:101
  54.9 82.9 %copy-start.3 = (f32[128,512]{1,0:T(8,128)}, f32[128,512]{1,0:T(8,128)S(1)}, u32[]{:S(2)}) copy-start(f32[128,512]{1,0:T(8,128)S(1)} %reduce_sum.126) | copy-start | bytes 786436
  99.6 235.3 %all-gather.5.cloned.1.call-start = ((), (), s32[]{:S(2)}) async-start(), calls=%async_computation.9 | async-start | bytes 4456448 | tf_op jit(solution)/shard_map/all_gather | solution.py:112
  137.8 150.7 %copy-start.2 = (f32[1,2,128,512]{3,2,1,0:T(8,128)S(1)}, f32[1,2,128,512]{3,2,1,0:T(8,128)}, u32[]{:S(2)}) copy-start(f32[1,2,128,512]{3,2,1,0:T(8,128)} %param.7) | copy-start | bytes 1572868
  138.9 18.6 %all-to-all-start = ((f32[4,128,512]{1,2,0:T(8,128)}), f32[4,128,512]{1,2,0:T(8,128)S(1)}, u32[]{:S(2)}, u32[]{:S(2)}) async-start(f32[4,128,512]{1,2,0:T(8,128)} %broadcast_in_dim.67), calls=%async_computation | async-start | bytes 2097152 | tf_op jit(solution)/shard_map/while/body/eval_jaxpr/all_to_all | solution.py:18
  163.6 17.3 %all-to-all-start = ((f32[4,128,512]{1,2,0:T(8,128)}), f32[4,128,512]{1,2,0:T(8,128)S(1)}, u32[]{:S(2)}, u32[]{:S(2)}) async-start(f32[4,128,512]{1,2,0:T(8,128)} %broadcast_in_dim.67), calls=%async_computation | async-start | bytes 2097152 | tf_op jit(solution)/shard_map/while/body/eval_jaxpr/all_to_all | solution.py:18
  186.8 16.4 %all-to-all-start = ((f32[4,128,512]{1,2,0:T(8,128)}), f32[4,128,512]{1,2,0:T(8,128)S(1)}, u32[]{:S(2)}, u32[]{:S(2)}) async-start(f32[4,128,512]{1,2,0:T(8,128)} %broadcast_in_dim.67), calls=%async_computation | async-start | bytes 2097152 | tf_op jit(solution)/shard_map/while/body/eval_jaxpr/all_to_all | solution.py:18
  209.2 15.2 %all-to-all-start = ((f32[4,128,512]{1,2,0:T(8,128)}), f32[4,128,512]{1,2,0:T(8,128)S(1)}, u32[]{:S(2)}, u32[]{:S(2)}) async-start(f32[4,128,512]{1,2,0:T(8,128)} %broadcast_in_dim.67), calls=%async_computation | async-start | bytes 2097152 | tf_op jit(solution)/shard_map/while/body/eval_jaxpr/all_to_all | solution.py:18
  230.4 14.1 %all-to-all-start = ((f32[4,128,512]{1,2,0:T(8,128)}), f32[4,128,512]{1,2,0:T(8,128)S(1)}, u32[]{:S(2)}, u32[]{:S(2)}) async-start(f32[4,128,512]{1,2,0:T(8,128)} %broadcast_in_dim.67), calls=%async_computation | async-start | bytes 2097152 | tf_op jit(solution)/shard_map/while/body/eval_jaxpr/all_to_all | solution.py:18
  250.5 13.2 %all-to-all-start = ((f32[4,128,512]{1,2,0:T(8,128)}), f32[4,128,512]{1,2,0:T(8,128)S(1)}, u32[]{:S(2)}, u32[]{:S(2)}) async-start(f32[4,128,512]{1,2,0:T(8,128)} %broadcast_in_dim.67), calls=%async_computation | async-start | bytes 2097152 | tf_op jit(solution)/shard_map/while/body/eval_jaxpr/all_to_all | solution.py:18
  269.7 13.2 %all-to-all-start = ((f32[4,128,512]{1,2,0:T(8,128)}), f32[4,128,512]{1,2,0:T(8,128)S(1)}, u32[]{:S(2)}, u32[]{:S(2)}) async-start(f32[4,128,512]{1,2,0:T(8,128)} %broadcast_in_dim.67), calls=%async_computation | async-start | bytes 2097152 | tf_op jit(solution)/shard_map/while/body/eval_jaxpr/all_to_all | solution.py:18
  287.8 0.7 copy-start
  311.9 28.7 %copy-start.1 = (f32[128,512]{1,0:T(8,128)S(1)}, f32[128,512]{1,0:T(8,128)}, u32[]{:S(2)}) copy-start(f32[128,512]{1,0:T(8,128)} %copy-done) | copy-start | bytes 786436
Sparse Core Ops, SparseCore 0:
  99.7 38.0 all-gather.2
  288.6 46.1 all-gather.4
where the time goes:
time: 381 us; the launch traced here: 379 us
  waiting for transfers between devices  156 us (41%)
  blocking collectives  105 us (28%)
  matrix products  39.3 us (10%)
  starting transfers between devices  33.3 us (9%)
  between operations  23.2 us (6%)
  local copies, waits for them, and re-layouts  14.4 us (4%)
  other arithmetic  7.74 us (2%)
    all_to_all x9, waiting for transfers between devices, sent_to_all(): return lax.all_to_all(copies, axis, split_axis=0, concat_axis=0, tiled=True)  95.2 us
    all_to_all x5, blocking collectives, sent_to_all(): return lax.all_to_all(copies, axis, split_axis=0, concat_axis=0, tiled=True)  66.7 us
    dot_general x8, matrix products, product(): jnp.dot(left, right, precision=HIGHEST, preferred_element_type=jnp.float32)  39.3 us
    all_gather x1, waiting for transfers between devices, shards(): columns = lax.all_gather(generator, ROW, axis=0, tiled=True)  38.1 us
    psum x4, blocking collectives, over_axes(): array = lax.psum(array, axis)  37.9 us
    all_to_all x9, starting transfers between devices, sent_to_all(): return lax.all_to_all(copies, axis, split_axis=0, concat_axis=0, tiled=True)  33.3 us
    all_gather x1, waiting for transfers between devices, shards(): expmap_cols = lax.all_gather(expmap, ROW, axis=0, tiled=True)  22.9 us
    broadcast_in_dim x14, local copies, waits for them, and re-layouts, sent_to_all(): copies = jnp.broadcast_to(array, (lax.axis_size(axis), *array.shape))  9.41 us
  transfers between devices with their start and end apart: 11, of which 11 were waited for; matrix products, arithmetic and copies ran while one was open for 2% of the time, Pallas kernels for 0%

commit v1 on v0

v1 whole, which is shorter than its diff:
```python
import functools
import math

import jax
import jax.numpy as jnp
from jax import lax
from jax.experimental import pallas as pl
from jax.experimental.pallas import tpu as pltpu
from jax.sharding import Mesh
from jax.sharding import PartitionSpec as P

ROW = ("zed", "core")
STEP_SCALE = 1.75
BLK = 128
MESH = pl.DeviceIdType.MESH

R177 = math.sqrt(177.0)
X3 = 2.0 / 3.0
X1 = X3 * (1.0 + R177) / 88.0
X2 = X3 * (1.0 + R177) / 352.0
X4 = (-271.0 + 29.0 * R177) / (315.0 * X3)
X5 = 11.0 * (-1.0 + R177) / (1260.0 * X3)
X6 = 11.0 * (-9.0 + R177) / (5040.0 * X3)
X7 = (89.0 - R177) / (5040.0 * X3 * X3)
Y2 = (857.0 - 58.0 * R177) / 630.0


def split(value):
    high = value.astype(jnp.bfloat16)
    low = (value - high.astype(jnp.float32)).astype(jnp.bfloat16)
    return high, low


def dot(left, right):
    return jnp.dot(left, right, preferred_element_type=jnp.float32)


def dot_split(left, right):
    (lh, ll), (rh, rl) = left, right
    return dot(lh, rh) + (dot(lh, rl) + dot(ll, rh))


def kernel(
    dims, idx_ref, tab_ref, m_ref, gp_ref, dp_ref,
    grad_ref, dir_ref, trial_ref, stat_ref,
    mall, dcm, drt, dsrc, gblk, blk2, blk4, eblk, etr, stile, sx, sz,
    drow, dcol, grow, gcol, acol, row2, col2, row4, col4, erow, ej, part, pz, px, qtile, ttile, tfin,
    a2a_s, a2a_r, dia_s, dia_r, dpr_s, dpr_r, row_s, row_r, col_s, col_r, fwd_s, fwd_r, one_s, one_r, sml_s, sml_r,
):
    nx, ny, nz, nk = dims
    count = nx * ny
    order = count * BLK
    wide = nx * BLK
    x, y = lax.axis_index("bvec"), lax.axis_index("col")
    z, k = lax.axis_index("zed"), lax.axis_index("core")
    r = nk * z + k
    c = nx * y + x

    def dev(xx, yy, zz, kk):
        return {"bvec": xx, "zed": zz, "core": kk, "col": yy}

    def off(value, step, size):
        return lax.rem(value + step, size) if step else value

    def lanes(index, size=BLK):
        return pl.ds(pl.multiple_of(index * size, size), size)

    plane = [(ox, oy) for ox in range(nx) for oy in range(ny) if (ox, oy) != (0, 0)]
    line = [(oz, ok) for oz in range(nz) for ok in range(nk)]
    others = line[1:]

    def at_plane(ox, oy):
        return dev(off(x, ox, nx), off(y, oy, ny), z, k)

    def at_line(oz, ok):
        return dev(x, y, off(z, oz, nz), off(k, ok, nk))

    px_t, py_t = lax.rem(r, nx), lax.div(r, nx)
    pz_t, pk_t = lax.div(c, nk), lax.rem(c, nk)
    off_diag = r != c
    holds = y == py_t

    barrier = pltpu.get_barrier_semaphore()
    for ox, oy in plane:
        pl.semaphore_signal(barrier, inc=1, device_id=at_plane(ox, oy), device_id_type=MESH)
    for oz, ok in others:
        pl.semaphore_signal(barrier, inc=1, device_id=at_line(oz, ok), device_id_type=MESH)

    @pl.when(off_diag)
    def _():
        pl.semaphore_signal(barrier, inc=1, device_id=dev(px_t, py_t, pz_t, pk_t), device_id_type=MESH)

    for b in range(nx):
        @pl.when((x != b) | off_diag)
        def _(b=b):
            pl.semaphore_signal(barrier, inc=1, device_id=dev(b, y, pz_t, pk_t), device_id_type=MESH)

    mall[pl.ds(x, 1)] = m_ref[:, :, lanes(x)][None]
    own_d = dp_ref[:, lanes(x)]
    eye_r = lax.broadcasted_iota(jnp.int32, (BLK, BLK), 0)
    eye_c = lax.broadcasted_iota(jnp.int32, (BLK, BLK), 1)
    eye = eye_r == eye_c
    dsrc[...] = jnp.zeros((8, BLK), jnp.float32)
    for p in range(2):
        dsrc[p:p + 1, :] = jnp.sum(jnp.where(eye, m_ref[p, :, lanes(px_t)], 0.0), axis=0, keepdims=True)
    if nx * 8 < BLK:
        dcm[nx * 8:, :] = jnp.zeros((BLK - nx * 8, BLK), jnp.float32)
    drow[:, lanes(y, wide)] = dp_ref[...]
    dcol[lanes(r), :] = own_d

    expected = len(plane) + len(others) + off_diag.astype(jnp.int32)
    asked = len(line) - (x == px_t).astype(jnp.int32)
    pl.semaphore_wait(barrier, expected + holds.astype(jnp.int32) * asked)

    def remote(src, dst, send, recv, device):
        return pltpu.make_async_remote_copy(
            src_ref=src, dst_ref=dst, send_sem=send, recv_sem=recv, device_id=device, device_id_type=MESH
        )

    dia_row = [
        remote(dsrc, dcm.at[pl.ds(pl.multiple_of(8 * x, 8), 8), :], dia_s.at[i], dia_r.at[x], at_plane(ox, oy))
        for i, (ox, oy) in enumerate(plane)
    ]
    dia_col = [
        remote(dsrc, drt.at[x], dia_s.at[len(plane) + i], dia_r.at[nx + x],
               dev(px_t, y, off(z, oz, nz), off(k, ok, nk)))
        for i, (oz, ok) in enumerate(line)
    ]

    @pl.when(holds)
    def _():
        for copy in dia_row:
            copy.start()
        for copy in dia_col[1:]:
            copy.start()
        dcm[pl.ds(pl.multiple_of(8 * x, 8), 8), :] = dsrc[...]

    @pl.when(holds & (x != px_t))
    def _():
        dia_col[0].start()

    @pl.when(jnp.logical_not(off_diag))
    def _():
        drt[pl.ds(x, 1)] = dsrc[...][None]

    a2a = []
    for ox in range(1, nx):
        xp = off(x, ox, nx)
        copy = remote(m_ref.at[:, :, lanes(xp)], mall.at[x], a2a_s.at[ox - 1], a2a_r.at[ox - 1], dev(xp, y, z, k))
        copy.start()
        a2a.append(copy)

    dprow = []
    for oy in range(1, ny):
        copy = remote(dp_ref, drow.at[:, lanes(y, wide)], dpr_s.at[oy - 1], dpr_r.at[oy - 1], at_plane(0, oy))
        copy.start()
        dprow.append(copy)

    def row_gather(stage, src, dst):
        copies = []
        for i, (ox, oy) in enumerate(plane):
            copy = remote(src, dst.at[:, lanes(c)], row_s.at[i], row_r.at[stage, i], at_plane(ox, oy))
            copy.start()
            copies.append(copy)
        return copies

    near = sorted(range(1, nz), key=lambda oz: (min(oz, nz - oz), oz))

    def line_gather(stage, src, slot):
        sends = {}
        for oz in near:
            sends[oz] = remote(src, slot(r), col_s.at[oz - 1], col_r.at[stage, oz - 1], at_line(oz, 0))
            sends[oz].start()
        forwards = [remote(src, slot(r), fwd_s.at[0], fwd_r.at[stage, 0], at_line(0, 1))]
        forwards[0].start()
        return sends, forwards, stage, slot

    def line_wait(state):
        sends, forwards, stage, slot = state
        for oz in near:
            sends[oz].wait_recv()
            held = slot(nk * off(z, nz - oz, nz) + k)
            copy = remote(held, held, fwd_s.at[oz], fwd_r.at[stage, oz], at_line(0, 1))
            copy.start()
            forwards.append(copy)
        for copy in forwards:
            copy.wait()
        for oz in near:
            sends[oz].wait_send()

    def column_slots(ref):
        return lambda index: ref.at[lanes(index), :]

    def row_slots(ref):
        return lambda index: ref.at[:, lanes(index)]

    dcol_state = line_gather(0, dp_ref.at[:, lanes(x)], column_slots(dcol))

    for b in range(nx):
        @pl.when(jnp.logical_not(holds & (x == b)))
        def _(b=b):
            slot = dcm.at[8 * b:8 * b + 8, :]
            remote(slot, slot, dia_s.at[0], dia_r.at[b], dev(x, y, z, k)).wait_recv()

        @pl.when(off_diag | (x != b))
        def _(b=b):
            slot = drt.at[b]
            remote(slot, slot, dia_s.at[0], dia_r.at[nx + b], dev(x, y, z, k)).wait_recv()

    weights = []
    for b in range(nx):
        value = jnp.float32(0.0)
        for t in range(tab_ref.shape[0]):
            value = value + jnp.where(idx_ref[b] == t, tab_ref[t], jnp.float32(0.0))
        weights.append(value)

    columns = jnp.transpose(dcm[...])
    for copy in a2a:
        copy.wait()
    total = jnp.zeros((BLK, BLK), jnp.float32)
    spread_row = jnp.zeros((1, BLK), jnp.float32)
    for b in range(nx):
        term = jnp.zeros((BLK, BLK), jnp.float32)
        for p in range(2):
            at_row = columns[:, 8 * b + p:8 * b + p + 1]
            at_col = drt[b, p:p + 1, :]
            term = term + mall[b, p] * (at_row - at_col)
        total = total + (2.0 * weights[b]) * term
        re_d, im_d = drt[b, 0:1, :], drt[b, 1:2, :]
        spread_row = spread_row + weights[b] * (1.0 - re_d * re_d - im_d * im_d)
    gblk[...] = total
    own_p = gp_ref[:, lanes(x)]
    first_line = (r == 0).astype(jnp.float32)
    stile[...] = jnp.zeros((8, BLK), jnp.float32)
    stile[0:1, :] = jnp.sum(total * total, axis=0, keepdims=True)
    stile[1:2, :] = jnp.sum(total * own_d, axis=0, keepdims=True)
    stile[2:3, :] = jnp.sum(own_d * own_d, axis=0, keepdims=True)
    stile[3:4, :] = jnp.sum(own_p * own_p, axis=0, keepdims=True)
    stile[4:5, :] = spread_row * first_line

    def small_plane(stage, src, dst):
        dst[pl.ds(c, 1)] = src[...][None]
        copies = []
        for i, (ox, oy) in enumerate(plane):
            copy = remote(src, dst.at[c], sml_s.at[i], sml_r.at[stage, i], at_plane(ox, oy))
            copy.start()
            copies.append(copy)
        return copies

    def small_line(stage, src, dst):
        dst[pl.ds(r, 1)] = src(r)[...][None]
        copies = []
        for i, (oz, ok) in enumerate(others):
            rp = nk * off(z, oz, nz) + off(k, ok, nk)
            copy = remote(src(rp), dst.at[r], sml_s.at[i], sml_r.at[stage, i], at_line(oz, ok))
            copy.start()
            copies.append(copy)
        return copies

    def wait_all(copies):
        for copy in copies:
            copy.wait()

    def summed(ref):
        value = ref[0]
        for i in range(1, count):
            value = value + ref[i]
        return value

    copies = small_plane(0, stile, sx)
    grow[:, lanes(c)] = total
    gcol[lanes(r), :] = total
    g_row = row_gather(0, gblk, grow)
    line_wait(dcol_state)
    g_col = line_gather(1, gblk, column_slots(gcol))
    wait_all(copies)
    stile[...] = summed(sx)
    copies = small_line(1, lambda index: stile, sz)
    wait_all(dprow)
    wait_all(copies)
    sums = jnp.broadcast_to(jnp.sum(summed(sz), axis=1, keepdims=True), (8, BLK))
    gg, gd, dd, pp = (sums[i:i + 1, :] for i in range(4))
    spread = sums[4:5, :] / order
    beta = gg / (1.0 + pp)
    norm = jnp.maximum(gg - 2.0 * beta * gd + beta * beta * dd, 0.0)
    scale = STEP_SCALE / jnp.sqrt(1.0 + norm / order)

    wait_all(g_row)
    line_wait(g_col)
    for j in range(nx):
        at = pl.ds(pl.multiple_of(y * wide + j * BLK, BLK), BLK)
        piece = grow[:, at]
        grad_ref[:, j * BLK:(j + 1) * BLK] = piece
        dir_ref[:, j * BLK:(j + 1) * BLK] = beta * drow[:, at] - piece

    chunk = 4 * BLK if order % (4 * BLK) == 0 else BLK
    beta_w = jnp.concatenate([beta] * (chunk // BLK), axis=1)
    scale_w = jnp.concatenate([scale] * (chunk // BLK), axis=1)

    acc = jnp.zeros((BLK, BLK), jnp.float32)
    for at in range(0, order, chunk):
        left = scale_w * (beta_w * drow[:, at:at + chunk] - grow[:, at:at + chunk])
        right = scale * (beta * dcol[at:at + chunk, :] - gcol[at:at + chunk, :])
        acol[at:at + chunk, :] = right
        acc = acc + dot_split(split(left), split(right))
    blk2[...] = acc
    row2[:, lanes(c)] = acc
    col2[lanes(r), :] = acc
    rows = row_gather(1, blk2, row2)
    cols = line_gather(2, blk2, column_slots(col2))
    wait_all(rows)
    line_wait(cols)

    acc = jnp.zeros((BLK, BLK), jnp.float32)
    for at in range(0, order, chunk):
        right = X1 * acol[at:at + chunk, :] + X2 * col2[at:at + chunk, :]
        acc = acc + dot_split(split(row2[:, at:at + chunk]), split(right))
    blk4[...] = acc
    row4[:, lanes(c)] = acc
    col4[lanes(r), :] = acc
    rows = row_gather(2, blk4, row4)
    cols = line_gather(3, blk4, column_slots(col4))
    wait_all(rows)
    line_wait(cols)

    acc = jnp.zeros((BLK, BLK), jnp.float32)
    for at in range(0, order, chunk):
        left = X3 * row2[:, at:at + chunk] + row4[:, at:at + chunk]
        right = X5 * acol[at:at + chunk, :] + X6 * col2[at:at + chunk, :] + X7 * col4[at:at + chunk, :]
        acc = acc + dot_split(split(left), split(right))
    acc = acc + X4 * (X3 * blk2[...] + blk4[...]) + Y2 * blk2[...] + acol[lanes(r), :]
    acc = acc + jnp.where(eye & jnp.logical_not(off_diag), 1.0, 0.0)
    eblk[...] = acc

    turn = remote(eblk, etr, one_s.at[0], one_r.at[0], dev(px_t, py_t, pz_t, pk_t))

    @pl.when(off_diag)
    def _():
        turn.start()

    erow[:, lanes(c)] = acc
    rows = row_gather(3, eblk, erow)

    @pl.when(off_diag)
    def _():
        turn.wait()

    @pl.when(jnp.logical_not(off_diag))
    def _():
        etr[...] = eblk[...]

    cols = line_gather(4, etr, row_slots(ej))
    ej[:, lanes(r)] = etr[...]
    pairs = [[split(mall[b, p]) for p in range(2)] for b in range(nx)]
    wait_all(rows)
    line_wait(cols)

    part[...] = jnp.zeros((8, order), jnp.float32)
    for at in range(0, order, chunk):
        right = split(ej[:, at:at + chunk])
        left = erow[:, at:at + chunk]
        for b in range(nx):
            for p in range(2):
                turned = dot_split(pairs[b][p], right)
                part[2 * b + p:2 * b + p + 1, at:at + chunk] = jnp.sum(left * turned, axis=0, keepdims=True)

    wait_all(small_line(2, lambda index: part.at[:, lanes(index)], pz))
    qtile[...] = summed(pz)
    wait_all(small_plane(3, qtile, px))
    sumt = summed(px)
    ttile[...] = sumt
    tfin[:, lanes(r)] = sumt
    copies = []
    for i, (oz, ok) in enumerate(others):
        copy = remote(ttile, tfin.at[:, lanes(r)], sml_s.at[i], sml_r.at[4, i], at_line(oz, ok))
        copy.start()
        copies.append(copy)

    @pl.when(holds)
    def _():
        for copy in dia_row:
            copy.wait_send()
        for copy in dia_col[1:]:
            copy.wait_send()

    @pl.when(holds & (x != px_t))
    def _():
        dia_col[0].wait_send()

    wait_all(copies)
    trial_ref[...] = tfin[...]
    trial = jnp.zeros((1, order), jnp.float32)
    for b in range(nx):
        re_t, im_t = tfin[2 * b:2 * b + 1, :], tfin[2 * b + 1:2 * b + 2, :]
        trial = trial + weights[b] * (1.0 - re_t * re_t - im_t * im_t)
    stat_ref[...] = jnp.zeros((8, BLK), jnp.float32)
    stat_ref[0:1, :] = spread
    stat_ref[1:2, :] = jnp.broadcast_to(jnp.sum(trial, axis=1, keepdims=True) / order, (1, BLK))


def shards(dims, m_matrices, bvec_index, weight_table, grad_prev, dir_prev):
    nx, ny, nz, nk = dims
    count = nx * ny
    order = count * BLK
    f32 = jnp.float32
    rows, cols = grad_prev.shape
    vmem = pl.BlockSpec(memory_space=pltpu.VMEM)
    smem = pl.BlockSpec(memory_space=pltpu.SMEM)
    wide = pltpu.VMEM((BLK, order), f32)
    tall = pltpu.VMEM((order, BLK), f32)
    block = pltpu.VMEM((BLK, BLK), f32)
    tile = pltpu.VMEM((8, BLK), f32)
    tiles = pltpu.VMEM((count, 8, BLK), f32)
    dma = pltpu.SemaphoreType.DMA
    n_plane, n_line = count - 1, nz * nk
    grad, direction, trial, stat = pl.pallas_call(
        functools.partial(kernel, dims),
        out_shape=(
            jax.ShapeDtypeStruct((rows, cols), f32),
            jax.ShapeDtypeStruct((rows, cols), f32),
            jax.ShapeDtypeStruct((8, order), f32),
            jax.ShapeDtypeStruct((8, BLK), f32),
        ),
        in_specs=[smem, smem, vmem, vmem, vmem],
        out_specs=(vmem, vmem, vmem, vmem),
        scratch_shapes=[
            pltpu.VMEM((nx, 2, BLK, BLK), f32), block, pltpu.VMEM((nx, 8, BLK), f32), tile,
            block, block, block, block, block, tile, tiles, tiles,
            wide, tall, wide, tall, tall, wide, tall, wide, tall, wide, wide,
            pltpu.VMEM((8, order), f32), tiles, tiles, tile, tile, pltpu.VMEM((8, order), f32),
            dma((nx - 1,)), dma((nx - 1,)),
            dma((n_plane + n_line,)), dma((2 * nx,)),
            dma((ny - 1,)), dma((ny - 1,)),
            dma((n_plane,)), dma((4, n_plane)),
            dma((nz - 1,)), dma((5, nz - 1)),
            dma((nz,)), dma((5, nz)),
            dma((1,)), dma((1,)),
            dma((n_plane,)), dma((5, n_plane)),
        ],
        compiler_params=pltpu.CompilerParams(
            collective_id=0, has_side_effects=True, vmem_limit_bytes=56 * 1024 * 1024
        ),
    )(bvec_index, weight_table, m_matrices.reshape(m_matrices.shape[1:]), grad_prev, dir_prev)
    return stat[0, 0], stat[1, 0], grad, direction, trial[: 2 * nx].reshape(nx, 2, order)


def solution(mesh):
    nx, ny, nk = mesh.shape["bvec"], mesh.shape["col"], 2
    nz = mesh.shape["row"] // nk
    torus = Mesh(mesh.devices.reshape(nx, nz, nk, ny), ("bvec", "zed", "core", "col"))
    return jax.shard_map(
        functools.partial(shards, (nx, ny, nz, nk)),
        mesh=torus,
        in_specs=(P("bvec", None, ROW, "col"), P(), P(), P(ROW, "col"), P(ROW, "col")),
        out_specs=(P(), P(), P(ROW, "col"), P(ROW, "col"), P()),
        check_vma=False,
    )
```

time: 381 us -> 135 us (0.35)
  waiting for transfers between devices: 156 us -> 0 us
  Pallas kernels: 0 us -> 129 us
  blocking collectives: 105 us -> 0 us
  matrix products: 39.3 us -> 0 us
  starting transfers between devices: 33.3 us -> 0 us
  between operations: 23.2 us -> 0.64 us
  local copies, waits for them, and re-layouts: 14.4 us -> 5.2 us
  other arithmetic: 7.74 us -> 0 us
    pallas_call x0 -> x1, Pallas kernels: none -> 129 us  [shards(): pl.pallas_call(functools.partial(kernel, dims), out_shape=(jax.ShapeDtype...]
    all_to_all x9 -> x0, waiting for transfers between devices: 95.2 us -> none  [sent_to_all(): return lax.all_to_all(copies, axis, split_axis=0, concat_axis=0, tiled=True)]
    all_to_all x5 -> x0, blocking collectives: 66.7 us -> none  [sent_to_all(): return lax.all_to_all(copies, axis, split_axis=0, concat_axis=0, tiled=True)]
    all_gather x2 -> x0, waiting for transfers between devices: 61 us -> none  [the longest x1 38.1 us: shards(): columns = lax.all_gather(generator, ROW, axis=0, tiled=True)]
    dot_general x8 -> x0, matrix products: 39.3 us -> none  [product(): jnp.dot(left, right, precision=HIGHEST, preferred_element_type=jnp.float32)]
    psum x4 -> x0, blocking collectives: 37.9 us -> none  [over_axes(): array = lax.psum(array, axis)]
    all_to_all x9 -> x0, starting transfers between devices: 33.3 us -> none  [sent_to_all(): return lax.all_to_all(copies, axis, split_axis=0, concat_axis=0, tiled=True)]
    broadcast_in_dim x14 -> x0, local copies, waits for them, and re-layouts: 9.41 us -> none  [sent_to_all(): copies = jnp.broadcast_to(array, (lax.axis_size(axis), *array.shape))]
  transfers between devices with their start and end apart: 11 -> 0, of which waited for: 11 -> 0; matrix products, arithmetic and copies ran while one was open for 2% -> 0% of each run, Pallas kernels for 0% -> 0%
where the time goes in v1:
time: 135 us
  Pallas kernels  129 us (96%)
  local copies, waits for them, and re-layouts  5.2 us (4%)
    pallas_call x1, Pallas kernels, shards(): pl.pallas_call(functools.partial(kernel, dims), out_shape=(jax.ShapeDtype...  129 us

profile of v1, /device:TPU:1, one launch (start us, length us, event | category | flops | bytes accessed | tf_op | source)
XLA Modules:
  0.0 135.3 jit_solution(7631670248405563485)
XLA Ops:
  0.6 129.5 %shard_map.92 = (f32[128,512]{1,0:T(8,128)}, f32[128,512]{1,0:T(8,128)}, f32[8,2048]{1,0:T(8,128)}, f32[8,128]{1,0:T(8,128)}) custom-call(s32[4]{0:T(128)} %idx_ref.1, f32[6]{0:T(128)} %tab_ref.1, f32[2,128,512]{2,1,0:T(8,128)} %bitcast.3, f32[128,512]{1,0:T(8,128)} %gp_ref.1, f32[128,512]{1,0:T(8,128)} %dp_ref.1), custom_call_target="tpu_custom_call" | custom-call | tf_op jit(solution)/shard_map/pallas_call | solution.py:416
  130.1 1.3 fusion
  131.4 1.5 %reshape.17 = f32[4,2,2048]{2,1,0:T(2,128)} reshape(f32[8,2048]{1,0:T(8,128)} %get-tuple-element.12) | data formatting | bytes 131072 | tf_op jit(solution)/shard_map/reshape | solution.py:444
  132.9 0.0 copy-start
  132.9 1.7 %copy.12 = f32[128,512]{1,0:T(8,128)} copy(f32[128,512]{1,0:T(8,128)} %get-tuple-element.22) | data formatting | bytes 524288
  134.6 0.0 copy-done
  134.6 0.7 copy.13
Async XLA Ops:
  132.9 1.7 %copy-start = (f32[128,512]{1,0:T(8,128)S(1)}, f32[128,512]{1,0:T(8,128)}, u32[]{:S(2)}) copy-start(f32[128,512]{1,0:T(8,128)} %get-tuple-element.23) | copy-start | bytes 786436

commit v2 on v1

--- a/solution.py
+++ b/solution.py
@@ -110,7 +110,8 @@
 
     expected = len(plane) + len(others) + off_diag.astype(jnp.int32)
     asked = len(line) - (x == px_t).astype(jnp.int32)
-    pl.semaphore_wait(barrier, expected + holds.astype(jnp.int32) * asked)
+    with jax.named_scope("barrier"):
+        pl.semaphore_wait(barrier, expected + holds.astype(jnp.int32) * asked)
 
     def remote(src, dst, send, recv, device):
         return pltpu.make_async_remote_copy(
@@ -150,54 +151,121 @@
         copy.start()
         a2a.append(copy)
 
+    def wait_all(copies, name="wait"):
+        with jax.named_scope(name):
+            for copy in copies:
+                copy.wait()
+
+    half = BLK // 2
+    top, low = slice(0, half), slice(half, BLK)
+
+    def far_block(step, part, index):
+        held = drow.at[part, lanes(off(y, ny - step, ny), wide)]
+        return remote(held, held, dpr_s.at[index], dpr_r.at[index], at_plane(0, step))
+
     dprow = []
-    for oy in range(1, ny):
-        copy = remote(dp_ref, drow.at[:, lanes(y, wide)], dpr_s.at[oy - 1], dpr_r.at[oy - 1], at_plane(0, oy))
+    for i, oy in enumerate((1, ny - 1)):
+        copy = remote(dp_ref, drow.at[:, lanes(y, wide)], dpr_s.at[i], dpr_r.at[i], at_plane(0, oy))
         copy.start()
         dprow.append(copy)
 
-    def row_gather(stage, src, dst):
-        copies = []
-        for i, (ox, oy) in enumerate(plane):
-            copy = remote(src, dst.at[:, lanes(c)], row_s.at[i], row_r.at[stage, i], at_plane(ox, oy))
+    ring_x = [1, nx - 1, 2]
+    ring_y = [1, ny - 1, 2]
+
+    def plane_start(stage, src, dst):
+        first = []
+        for i, ox in enumerate(ring_x):
+            first.append(remote(src, dst.at[:, lanes(c)], row_s.at[i], row_r.at[stage, i], at_plane(ox, 0)))
+            first.append(remote(src, dst.at[:, lanes(c)], row_s.at[3 + i], row_r.at[stage, 3 + i], at_plane(0, ring_y[i])))
+        for copy in first:
             copy.start()
-            copies.append(copy)
-        return copies
-
-    near = sorted(range(1, nz), key=lambda oz: (min(oz, nz - oz), oz))
-
-    def line_gather(stage, src, slot):
-        sends = {}
-        for oz in near:
-            sends[oz] = remote(src, slot(r), col_s.at[oz - 1], col_r.at[stage, oz - 1], at_line(oz, 0))
-            sends[oz].start()
-        forwards = [remote(src, slot(r), fwd_s.at[0], fwd_r.at[stage, 0], at_line(0, 1))]
-        forwards[0].start()
-        return sends, forwards, stage, slot
-
-    def line_wait(state):
-        sends, forwards, stage, slot = state
-        for oz in near:
-            sends[oz].wait_recv()
-            held = slot(nk * off(z, nz - oz, nz) + k)
-            copy = remote(held, held, fwd_s.at[oz], fwd_r.at[stage, oz], at_line(0, 1))
-            copy.start()
-            forwards.append(copy)
-        for copy in forwards:
-            copy.wait()
-        for oz in near:
-            sends[oz].wait_send()
+        return stage, dst, first, []
+
+    def plane_forward(state):
+        stage, dst, first, second = state
+        with jax.named_scope(f"row{stage}a"):
+            for i in range(3):
+                first[2 * i].wait_recv()
+                held = dst.at[top, lanes(nx * y + off(x, nx - ring_x[i], nx))]
+                for j in range(3):
+                    at = 6 + 3 * i + j
+                    second.append(remote(held, held, row_s.at[at], row_r.at[stage, at], at_plane(0, ring_y[j])))
+                    second[-1].start()
+                first[2 * i + 1].wait_recv()
+                held = dst.at[low, lanes(nx * off(y, ny - ring_y[i], ny) + x)]
+                for j in range(3):
+                    at = 15 + 3 * i + j
+                    second.append(remote(held, held, row_s.at[at], row_r.at[stage, at], at_plane(ring_x[j], 0)))
+                    second[-1].start()
+
+    def plane_finish(state):
+        stage, _, first, second = state
+        with jax.named_scope(f"row{stage}b"):
+            for copy in second:
+                copy.wait()
+            for copy in first:
+                copy.wait_send()
+
+    def line_start(stage, src, slot):
+        bank = 1 if stage == 0 else 0
+        first = {}
+        for i, oz in enumerate((1, nz - 1, 2, nz - 2)):
+            first[oz] = remote(src, slot(r), col_s.at[bank, i], col_r.at[stage, i], at_line(oz, 0))
+            first[oz].start()
+        over = [remote(src, slot(r), fwd_s.at[bank, 0], fwd_r.at[stage, 0], at_line(0, 1))]
+        over[0].start()
+        return stage, bank, slot, first, {}, over
+
+    def line_across(state, oz):
+        stage, bank, slot, first, second, over = state
+        held = slot(nk * off(z, nz - oz, nz) + k)
+        over.append(remote(held, held, fwd_s.at[bank, oz], fwd_r.at[stage, oz], at_line(0, 1)))
+        over[-1].start()
+
+    def line_forward(state):
+        stage, bank, slot, first, second, over = state
+        with jax.named_scope(f"line{stage}a"):
+            for i, (oz, step, part) in enumerate(((2, 1, top), (nz - 2, nz - 1, low))):
+                first[oz].wait_recv()
+                held = slot(nk * off(z, nz - oz, nz) + k)
+                second[i] = remote(held, held, col_s.at[bank, 4 + i], col_r.at[stage, 4 + i], at_line(step, 0))
+                second[i].start()
+                held = slot(nk * off(z, nz - oz, nz) + k, part)
+                second[2 + i] = remote(held, held, col_s.at[bank, 6 + i], col_r.at[stage, 6 + i], at_line(oz, 0))
+                second[2 + i].start()
+            for oz in (1, nz - 1, 2, nz - 2):
+                if oz in (1, nz - 1):
+                    first[oz].wait_recv()
+                line_across(state, oz)
+
+    def line_finish(state):
+        stage, bank, slot, first, second, over = state
+        with jax.named_scope(f"line{stage}b"):
+            second[0].wait_recv()
+            line_across(state, 3)
+            second[1].wait_recv()
+            line_across(state, nz - 3)
+            second[2].wait_recv()
+            second[3].wait_recv()
+            line_across(state, 4)
+            for copy in over:
+                copy.wait()
+            for copy in list(first.values()) + list(second.values()):
+                copy.wait_send()
 
     def column_slots(ref):
-        return lambda index: ref.at[lanes(index), :]
+        def slot(index, part=slice(0, BLK)):
+            return ref.at[pl.ds(pl.multiple_of(index * BLK + part.start, half), part.stop - part.start), :]
+        return slot
 
     def row_slots(ref):
-        return lambda index: ref.at[:, lanes(index)]
-
-    dcol_state = line_gather(0, dp_ref.at[:, lanes(x)], column_slots(dcol))
+        return lambda index, part=slice(0, BLK): ref.at[part, lanes(index)]
+
+    d_col = line_start(0, dp_ref.at[:, lanes(x)], column_slots(dcol))
 
     for b in range(nx):
         @pl.when(jnp.logical_not(holds & (x == b)))
+        @jax.named_scope("diag_r")
         def _(b=b):
             slot = dcm.at[8 * b:8 * b + 8, :]
             remote(slot, slot, dia_s.at[0], dia_r.at[b], dev(x, y, z, k)).wait_recv()
@@ -215,8 +283,13 @@
         weights.append(value)
 
     columns = jnp.transpose(dcm[...])
-    for copy in a2a:
-        copy.wait()
+    line_forward(d_col)
+    far = []
+    for i, (step, piece) in enumerate(((1, top), (ny - 1, low))):
+        dprow[i].wait_recv()
+        far.append(far_block(step, piece, 2 + i))
+        far[-1].start()
+    wait_all(a2a, "a2a")
     total = jnp.zeros((BLK, BLK), jnp.float32)
     spread_row = jnp.zeros((1, BLK), jnp.float32)
     for b in range(nx):
@@ -257,27 +330,29 @@
             copies.append(copy)
         return copies
 
-    def wait_all(copies):
-        for copy in copies:
-            copy.wait()
-
     def summed(ref):
         value = ref[0]
         for i in range(1, count):
             value = value + ref[i]
         return value
 
-    copies = small_plane(0, stile, sx)
+    copies = small_line(0, lambda index: stile, sx)
     grow[:, lanes(c)] = total
     gcol[lanes(r), :] = total
-    g_row = row_gather(0, gblk, grow)
-    line_wait(dcol_state)
-    g_col = line_gather(1, gblk, column_slots(gcol))
-    wait_all(copies)
+    rows = plane_start(0, gblk, grow)
+    cols = line_start(1, gblk, column_slots(gcol))
+    line_finish(d_col)
+    plane_forward(rows)
+    line_forward(cols)
+    wait_all(copies, "small0")
     stile[...] = summed(sx)
-    copies = small_line(1, lambda index: stile, sz)
-    wait_all(dprow)
-    wait_all(copies)
+    copies = small_plane(1, stile, sz)
+    wait_all(far, "far")
+    for copy in dprow:
+        copy.wait_send()
+    line_finish(cols)
+    plane_finish(rows)
+    wait_all(copies, "small1")
     sums = jnp.broadcast_to(jnp.sum(summed(sz), axis=1, keepdims=True), (8, BLK))
     gg, gd, dd, pp = (sums[i:i + 1, :] for i in range(4))
     spread = sums[4:5, :] / order
@@ -285,8 +360,6 @@
     norm = jnp.maximum(gg - 2.0 * beta * gd + beta * beta * dd, 0.0)
     scale = STEP_SCALE / jnp.sqrt(1.0 + norm / order)
 
-    wait_all(g_row)
-    line_wait(g_col)
     for j in range(nx):
         at = pl.ds(pl.multiple_of(y * wide + j * BLK, BLK), BLK)
         piece = grow[:, at]
@@ -306,10 +379,12 @@
     blk2[...] = acc
     row2[:, lanes(c)] = acc
     col2[lanes(r), :] = acc
-    rows = row_gather(1, blk2, row2)
-    cols = line_gather(2, blk2, column_slots(col2))
-    wait_all(rows)
-    line_wait(cols)
+    rows = plane_start(1, blk2, row2)
+    cols = line_start(2, blk2, column_slots(col2))
+    line_forward(cols)
+    plane_forward(rows)
+    line_finish(cols)
+    plane_finish(rows)
 
     acc = jnp.zeros((BLK, BLK), jnp.float32)
     for at in range(0, order, chunk):
@@ -318,10 +393,12 @@
     blk4[...] = acc
     row4[:, lanes(c)] = acc
     col4[lanes(r), :] = acc
-    rows = row_gather(2, blk4, row4)
-    cols = line_gather(3, blk4, column_slots(col4))
-    wait_all(rows)
-    line_wait(cols)
+    rows = plane_start(2, blk4, row4)
+    cols = line_start(3, blk4, column_slots(col4))
+    line_forward(cols)
+    plane_forward(rows)
+    line_finish(cols)
+    plane_finish(rows)
 
     acc = jnp.zeros((BLK, BLK), jnp.float32)
     for at in range(0, order, chunk):
@@ -339,21 +416,24 @@
         turn.start()
 
     erow[:, lanes(c)] = acc
-    rows = row_gather(3, eblk, erow)
+    rows = plane_start(3, eblk, erow)
 
     @pl.when(off_diag)
     def _():
-        turn.wait()
+        with jax.named_scope("turn"):
+            turn.wait()
 
     @pl.when(jnp.logical_not(off_diag))
     def _():
         etr[...] = eblk[...]
 
-    cols = line_gather(4, etr, row_slots(ej))
+    cols = line_start(4, etr, row_slots(ej))
     ej[:, lanes(r)] = etr[...]
     pairs = [[split(mall[b, p]) for p in range(2)] for b in range(nx)]
-    wait_all(rows)
-    line_wait(cols)
+    plane_forward(rows)
+    line_forward(cols)
+    line_finish(cols)
+    plane_finish(rows)
 
     part[...] = jnp.zeros((8, order), jnp.float32)
     for at in range(0, order, chunk):
@@ -364,9 +444,9 @@
                 turned = dot_split(pairs[b][p], right)
                 part[2 * b + p:2 * b + p + 1, at:at + chunk] = jnp.sum(left * turned, axis=0, keepdims=True)
 
-    wait_all(small_line(2, lambda index: part.at[:, lanes(index)], pz))
+    wait_all(small_line(2, lambda index: part.at[:, lanes(index)], pz), "small2")
     qtile[...] = summed(pz)
-    wait_all(small_plane(3, qtile, px))
+    wait_all(small_plane(3, qtile, px), "small3")
     sumt = summed(px)
     ttile[...] = sumt
     tfin[:, lanes(r)] = sumt
@@ -387,7 +467,7 @@
     def _():
         dia_col[0].wait_send()
 
-    wait_all(copies)
+    wait_all(copies, "small4")
     trial_ref[...] = tfin[...]
     trial = jnp.zeros((1, order), jnp.float32)
     for b in range(nx):
@@ -430,10 +510,10 @@
             pltpu.VMEM((8, order), f32), tiles, tiles, tile, tile, pltpu.VMEM((8, order), f32),
             dma((nx - 1,)), dma((nx - 1,)),
             dma((n_plane + n_line,)), dma((2 * nx,)),
-            dma((ny - 1,)), dma((ny - 1,)),
-            dma((n_plane,)), dma((4, n_plane)),
-            dma((nz - 1,)), dma((5, nz - 1)),
-            dma((nz,)), dma((5, nz)),
+            dma((4,)), dma((4,)),
+            dma((24,)), dma((4, 24)),
+            dma((2, 8)), dma((5, 8)),
+            dma((2, nz)), dma((5, nz)),
             dma((1,)), dma((1,)),
             dma((n_plane,)), dma((5, n_plane)),
         ],

time: 135 us -> 118 us (0.87)
  Pallas kernels: 129 us -> 112 us
    pallas_call x1, Pallas kernels: 129 us -> 112 us  [shards(): pl.pallas_call(functools.partial(kernel, dims), out_shape=(jax.ShapeDtype...]
where the time goes in v2:
time: 118 us; the launch traced here: 117 us
  Pallas kernels  112 us (95%)
  local copies, waits for them, and re-layouts  5.2 us (4%)
    pallas_call x1, Pallas kernels, shards(): pl.pallas_call(functools.partial(kernel, dims), out_shape=(jax.ShapeDtype...  112 us
    unnamed x4, local copies, waits for them, and re-layouts  2.42 us

profile of v2, /device:TPU:1, one launch (start us, length us, event | category | flops | bytes accessed | tf_op | source)
XLA Modules:
  0.0 117.4 jit_solution(6295844931759958289)
XLA Ops:
  0.6 111.5 %shard_map.92 = (f32[128,512]{1,0:T(8,128)}, f32[128,512]{1,0:T(8,128)}, f32[8,2048]{1,0:T(8,128)}, f32[8,128]{1,0:T(8,128)}) custom-call(s32[4]{0:T(128)} %idx_ref.1, f32[6]{0:T(128)} %tab_ref.1, f32[2,128,512]{2,1,0:T(8,128)} %bitcast.3, f32[128,512]{1,0:T(8,128)} %gp_ref.1, f32[128,512]{1,0:T(8,128)} %dp_ref.1), custom_call_target="tpu_custom_call" | custom-call | tf_op jit(solution)/shard_map/pallas_call | solution.py:496
  112.2 1.3 %fusion = (f32[1,1]{1,0:T(1,128)}, f32[1,1]{1,0:T(1,128)}) fusion(f32[8,128]{1,0:T(8,128)} %get-tuple-element.9), kind=kLoop, calls=%fused_computation | loop fusion | bytes 16 | tf_op jit(solution)/shard_map/slice | solution.py:524
  113.4 1.5 %reshape.17 = f32[4,2,2048]{2,1,0:T(2,128)} reshape(f32[8,2048]{1,0:T(8,128)} %get-tuple-element.12) | data formatting | bytes 131072 | tf_op jit(solution)/shard_map/reshape | solution.py:524
  114.9 0.0 copy-start
  115.0 1.7 %copy.12 = f32[128,512]{1,0:T(8,128)} copy(f32[128,512]{1,0:T(8,128)} %get-tuple-element.22) | data formatting | bytes 524288
  116.7 0.0 copy-done
  116.7 0.7 copy.13
Async XLA Ops:
  114.9 1.7 %copy-start = (f32[128,512]{1,0:T(8,128)S(1)}, f32[128,512]{1,0:T(8,128)}, u32[]{:S(2)}) copy-start(f32[128,512]{1,0:T(8,128)} %get-tuple-element.23) | copy-start | bytes 786436

commit v3 on v2

--- a/solution.py
+++ b/solution.py
@@ -37,15 +37,18 @@
 
 def dot_split(left, right):
     (lh, ll), (rh, rl) = left, right
-    return dot(lh, rh) + (dot(lh, rl) + dot(ll, rh))
+    size = rh.shape[1]
+    both = dot(lh, jnp.concatenate([rh, rl], axis=1))
+    return both[:, :size] + (both[:, size:] + dot(ll, rh))
 
 
 def kernel(
-    dims, idx_ref, tab_ref, m_ref, gp_ref, dp_ref,
-    grad_ref, dir_ref, trial_ref, stat_ref,
+    dims, m_in, dp_in, gp_in, idx_in, tab_in,
+    grad_ref, dir_ref, tfin, stat_ref,
+    idx_ref, tab_ref, m_ref, gp_ref, dp_ref, in_s,
     mall, dcm, drt, dsrc, gblk, blk2, blk4, eblk, etr, stile, sx, sz,
-    drow, dcol, grow, gcol, acol, row2, col2, row4, col4, erow, ej, part, pz, px, qtile, ttile, tfin,
-    a2a_s, a2a_r, dia_s, dia_r, dpr_s, dpr_r, row_s, row_r, col_s, col_r, fwd_s, fwd_r, one_s, one_r, sml_s, sml_r,
+    drow, dcol, grow, gcol, acol, row2, col2, row4, col4, erow, ej, mt, turned, part, pz, px, qtile, ttile,
+    a2a_s, a2a_r, dia_s, dia_r, dpr_s, dpr_r, row_s, row_r, col_s, col_r, fwd_s, fwd_r, one_s, one_r, sml_s, sml_r, pz_s, pz_r,
 ):
     nx, ny, nz, nk = dims
     count = nx * ny
@@ -80,20 +83,28 @@
     off_diag = r != c
     holds = y == py_t
 
+    loads = [
+        pltpu.make_async_copy(src, dst, in_s.at[i])
+        for i, (src, dst) in enumerate(
+            ((m_in, m_ref), (dp_in, dp_ref), (gp_in, gp_ref), (idx_in, idx_ref), (tab_in, tab_ref))
+        )
+    ]
+    for copy in loads:
+        copy.start()
+
     barrier = pltpu.get_barrier_semaphore()
     for ox, oy in plane:
         pl.semaphore_signal(barrier, inc=1, device_id=at_plane(ox, oy), device_id_type=MESH)
     for oz, ok in others:
         pl.semaphore_signal(barrier, inc=1, device_id=at_line(oz, ok), device_id_type=MESH)
 
-    @pl.when(off_diag)
-    def _():
-        pl.semaphore_signal(barrier, inc=1, device_id=dev(px_t, py_t, pz_t, pk_t), device_id_type=MESH)
-
     for b in range(nx):
         @pl.when((x != b) | off_diag)
         def _(b=b):
             pl.semaphore_signal(barrier, inc=1, device_id=dev(b, y, pz_t, pk_t), device_id_type=MESH)
+
+    for copy in loads:
+        copy.wait()
 
     mall[pl.ds(x, 1)] = m_ref[:, :, lanes(x)][None]
     own_d = dp_ref[:, lanes(x)]
@@ -108,7 +119,7 @@
     drow[:, lanes(y, wide)] = dp_ref[...]
     dcol[lanes(r), :] = own_d
 
-    expected = len(plane) + len(others) + off_diag.astype(jnp.int32)
+    expected = len(plane) + len(others)
     asked = len(line) - (x == px_t).astype(jnp.int32)
     with jax.named_scope("barrier"):
         pl.semaphore_wait(barrier, expected + holds.astype(jnp.int32) * asked)
@@ -209,7 +220,7 @@
     def line_start(stage, src, slot):
         bank = 1 if stage == 0 else 0
         first = {}
-        for i, oz in enumerate((1, nz - 1, 2, nz - 2)):
+        for i, oz in enumerate((2, nz - 2, 1, nz - 1)):
             first[oz] = remote(src, slot(r), col_s.at[bank, i], col_r.at[stage, i], at_line(oz, 0))
             first[oz].start()
         over = [remote(src, slot(r), fwd_s.at[bank, 0], fwd_r.at[stage, 0], at_line(0, 1))]
@@ -233,7 +244,11 @@
                 held = slot(nk * off(z, nz - oz, nz) + k, part)
                 second[2 + i] = remote(held, held, col_s.at[bank, 6 + i], col_r.at[stage, 6 + i], at_line(oz, 0))
                 second[2 + i].start()
-            for oz in (1, nz - 1, 2, nz - 2):
+
+    def line_near(state):
+        stage, bank, slot, first, second, over = state
+        with jax.named_scope(f"line{stage}n"):
+            for oz in (2, nz - 2, 1, nz - 1):
                 if oz in (1, nz - 1):
                     first[oz].wait_recv()
                 line_across(state, oz)
@@ -284,6 +299,7 @@
 
     columns = jnp.transpose(dcm[...])
     line_forward(d_col)
+    line_near(d_col)
     far = []
     for i, (step, piece) in enumerate(((1, top), (ny - 1, low))):
         dprow[i].wait_recv()
@@ -341,9 +357,10 @@
     gcol[lanes(r), :] = total
     rows = plane_start(0, gblk, grow)
     cols = line_start(1, gblk, column_slots(gcol))
+    line_forward(cols)
+    plane_forward(rows)
+    line_near(cols)
     line_finish(d_col)
-    plane_forward(rows)
-    line_forward(cols)
     wait_all(copies, "small0")
     stile[...] = summed(sx)
     copies = small_plane(1, stile, sz)
@@ -381,8 +398,14 @@
     col2[lanes(r), :] = acc
     rows = plane_start(1, blk2, row2)
     cols = line_start(2, blk2, column_slots(col2))
+    for b in range(nx):
+        for p in range(2):
+            i = 2 * b + p
+            high, tail = split(jnp.transpose(mall[b, p]))
+            mt[i * BLK:(i + 1) * BLK, :] = jnp.concatenate([high, tail], axis=1)
     line_forward(cols)
     plane_forward(rows)
+    line_near(cols)
     line_finish(cols)
     plane_finish(rows)
 
@@ -395,15 +418,19 @@
     col4[lanes(r), :] = acc
     rows = plane_start(2, blk4, row4)
     cols = line_start(3, blk4, column_slots(col4))
+    for at in range(0, order, chunk):
+        grow[:, at:at + chunk] = X3 * row2[:, at:at + chunk]
+        gcol[at:at + chunk, :] = X5 * acol[at:at + chunk, :] + X6 * col2[at:at + chunk, :]
     line_forward(cols)
     plane_forward(rows)
+    line_near(cols)
     line_finish(cols)
     plane_finish(rows)
 
     acc = jnp.zeros((BLK, BLK), jnp.float32)
     for at in range(0, order, chunk):
-        left = X3 * row2[:, at:at + chunk] + row4[:, at:at + chunk]
-        right = X5 * acol[at:at + chunk, :] + X6 * col2[at:at + chunk, :] + X7 * col4[at:at + chunk, :]
+        left = grow[:, at:at + chunk] + row4[:, at:at + chunk]
+        right = gcol[at:at + chunk, :] + X7 * col4[at:at + chunk, :]
         acc = acc + dot_split(split(left), split(right))
     acc = acc + X4 * (X3 * blk2[...] + blk4[...]) + Y2 * blk2[...] + acol[lanes(r), :]
     acc = acc + jnp.where(eye & jnp.logical_not(off_diag), 1.0, 0.0)
@@ -429,22 +456,34 @@
 
     cols = line_start(4, etr, row_slots(ej))
     ej[:, lanes(r)] = etr[...]
-    pairs = [[split(mall[b, p]) for p in range(2)] for b in range(nx)]
     plane_forward(rows)
     line_forward(cols)
+    line_near(cols)
+    plane_finish(rows)
+    for at in range(0, order, chunk):
+        high, tail = split(erow[:, at:at + chunk])
+        turned[:, at:at + chunk] = dot(mt[...], jnp.concatenate([high, high], axis=0)) + dot(mt[:, :BLK], tail)
     line_finish(cols)
-    plane_finish(rows)
-
-    part[...] = jnp.zeros((8, order), jnp.float32)
+
+    def to_owner(j):
+        return remote(part.at[:, j * BLK:(j + 1) * BLK], pz.at[r], pz_s.at[j], pz_r.at[r], dev(x, y, j // nk, j % nk))
+
     for at in range(0, order, chunk):
-        right = split(ej[:, at:at + chunk])
-        left = erow[:, at:at + chunk]
-        for b in range(nx):
-            for p in range(2):
-                turned = dot_split(pairs[b][p], right)
-                part[2 * b + p:2 * b + p + 1, at:at + chunk] = jnp.sum(left * turned, axis=0, keepdims=True)
-
-    wait_all(small_line(2, lambda index: part.at[:, lanes(index)], pz), "small2")
+        left = ej[:, at:at + chunk]
+        for i in range(2 * nx):
+            part[i:i + 1, at:at + chunk] = jnp.sum(
+                left * turned[i * BLK:(i + 1) * BLK, at:at + chunk], axis=0, keepdims=True
+            )
+        for j in range(at // BLK, (at + chunk) // BLK):
+            @pl.when(r != j)
+            def _(j=j):
+                to_owner(j).start()
+
+    pz[pl.ds(r, 1)] = part[:, lanes(r)][None]
+    with jax.named_scope("small2"):
+        for oz, ok in others:
+            rp = nk * off(z, oz, nz) + off(k, ok, nk)
+            remote(pz.at[rp], pz.at[rp], pz_s.at[0], pz_r.at[rp], at_line(oz, ok)).wait_recv()
     qtile[...] = summed(pz)
     wait_all(small_plane(3, qtile, px), "small3")
     sumt = summed(px)
@@ -467,8 +506,12 @@
     def _():
         dia_col[0].wait_send()
 
+    for j in range(count):
+        @pl.when(r != j)
+        def _(j=j):
+            to_owner(j).wait_send()
+
     wait_all(copies, "small4")
-    trial_ref[...] = tfin[...]
     trial = jnp.zeros((1, order), jnp.float32)
     for b in range(nx):
         re_t, im_t = tfin[2 * b:2 * b + 1, :], tfin[2 * b + 1:2 * b + 2, :]
@@ -476,6 +519,15 @@
     stat_ref[...] = jnp.zeros((8, BLK), jnp.float32)
     stat_ref[0:1, :] = spread
     stat_ref[1:2, :] = jnp.broadcast_to(jnp.sum(trial, axis=1, keepdims=True) / order, (1, BLK))
+
+
+def hand_out(grad_ref, dir_ref, trial_ref, stat_ref, spread_out, trial_spread_out, grad_out, dir_out, trial_out):
+    spread_out[0, 0] = jnp.sum(stat_ref[0:1, 0:1])
+    trial_spread_out[0, 0] = jnp.sum(stat_ref[1:2, 0:1])
+    grad_out[...] = grad_ref[...]
+    dir_out[...] = dir_ref[...]
+    for b in range(trial_out.shape[0]):
+        trial_out[b] = trial_ref[2 * b:2 * b + 2, :]
 
 
 def shards(dims, m_matrices, bvec_index, weight_table, grad_prev, dir_prev):
@@ -501,13 +553,16 @@
             jax.ShapeDtypeStruct((8, order), f32),
             jax.ShapeDtypeStruct((8, BLK), f32),
         ),
-        in_specs=[smem, smem, vmem, vmem, vmem],
+        in_specs=[pl.BlockSpec(memory_space=pltpu.HBM)] * 5,
         out_specs=(vmem, vmem, vmem, vmem),
         scratch_shapes=[
+            pltpu.SMEM(bvec_index.shape, jnp.int32), pltpu.SMEM(weight_table.shape, f32),
+            pltpu.VMEM(m_matrices.shape[1:], f32), pltpu.VMEM((rows, cols), f32), pltpu.VMEM((rows, cols), f32), dma((5,)),
             pltpu.VMEM((nx, 2, BLK, BLK), f32), block, pltpu.VMEM((nx, 8, BLK), f32), tile,
             block, block, block, block, block, tile, tiles, tiles,
             wide, tall, wide, tall, tall, wide, tall, wide, tall, wide, wide,
-            pltpu.VMEM((8, order), f32), tiles, tiles, tile, tile, pltpu.VMEM((8, order), f32),
+            pltpu.VMEM((2 * nx * BLK, 2 * BLK), jnp.bfloat16), pltpu.VMEM((2 * nx * BLK, order), f32),
+            pltpu.VMEM((8, order), f32), tiles, tiles, tile, tile,
             dma((nx - 1,)), dma((nx - 1,)),
             dma((n_plane + n_line,)), dma((2 * nx,)),
             dma((4,)), dma((4,)),
@@ -515,13 +570,25 @@
             dma((2, 8)), dma((5, 8)),
             dma((2, nz)), dma((5, nz)),
             dma((1,)), dma((1,)),
-            dma((n_plane,)), dma((5, n_plane)),
+            dma((n_plane,)), dma((5, n_plane)), dma((count,)), dma((count,)),
         ],
         compiler_params=pltpu.CompilerParams(
-            collective_id=0, has_side_effects=True, vmem_limit_bytes=56 * 1024 * 1024
+            collective_id=0, has_side_effects=True, vmem_limit_bytes=40 * 1024 * 1024
         ),
-    )(bvec_index, weight_table, m_matrices.reshape(m_matrices.shape[1:]), grad_prev, dir_prev)
-    return stat[0, 0], stat[1, 0], grad, direction, trial[: 2 * nx].reshape(nx, 2, order)
+    )(*(
+        pltpu.with_memory_space_constraint(array, pltpu.HBM)
+        for array in (m_matrices.reshape(m_matrices.shape[1:]), dir_prev, grad_prev, bvec_index, weight_table)
+    ))
+    one = jax.ShapeDtypeStruct((1, 1), f32)
+    block_out = jax.ShapeDtypeStruct((rows, cols), f32)
+    spread, trial_spread, grad, direction, trial = pl.pallas_call(
+        hand_out,
+        out_shape=(one, one, block_out, block_out, jax.ShapeDtypeStruct((nx, 2, order), f32)),
+        in_specs=[vmem] * 4,
+        out_specs=(smem, smem, vmem, vmem, vmem),
+        compiler_params=pltpu.CompilerParams(vmem_limit_bytes=8 * 1024 * 1024),
+    )(grad, direction, trial, stat)
+    return spread.reshape(()), trial_spread.reshape(()), grad, direction, trial
 
 
 def solution(mesh):

time: 118 us -> 102 us (0.86)
  Pallas kernels: 112 us -> 101 us
  local copies, waits for them, and re-layouts: 5.2 us -> 0 us
    pallas_call x1, Pallas kernels: 112 us -> 101 us  [shards(): pl.pallas_call(functools.partial(kernel, dims), out_shape=(jax.ShapeDtype...]
    unnamed x4 -> x0, local copies, waits for them, and re-layouts: 2.42 us -> none
    reshape x1 -> x0, local copies, waits for them, and re-layouts: 1.51 us -> none  [shards(): trial[:2 * nx].reshape(nx, 2, order)]
    slice x1 -> x0, local copies, waits for them, and re-layouts: 1.27 us -> none  [shards(): stat[1, 0]]
where the time goes in v3:
time: 102 us
  Pallas kernels  101 us (99%)
    pallas_call x1, Pallas kernels, shards(): pl.pallas_call(functools.partial(kernel, dims), out_shape=(jax.ShapeDtype...  101 us

profile of v3, /device:TPU:1, one launch (start us, length us, event | category | flops | bytes accessed | tf_op | source)
XLA Modules:
  0.0 102.1 jit_solution(7867814297837869774)
XLA Ops:
  0.6 100.6 %shard_map.92 = (f32[128,512]{1,0:T(8,128)S(1)}, f32[128,512]{1,0:T(8,128)S(1)}, f32[8,2048]{1,0:T(8,128)S(1)}, f32[8,128]{1,0:T(8,128)S(1)}) custom-call(f32[2,128,512]{2,1,0:T(8,128)} %bitcast.3, f32[128,512]{1,0:T(8,128)} %dp_in.1, f32[128,512]{1,0:T(8,128)} %gp_in.1, s32[4]{0:T(128)} %idx_in.1, f32[6]{0:T(128)} %tab_in.1), custom_call_target="tpu_custom_call" | custom-call | tf_op jit(solution)/shard_map/pallas_call | solution.py:548
  101.3 0.8 shard_map.93

commit v4 on v3

--- a/solution.py
+++ b/solution.py
@@ -1,5 +1,4 @@
 import functools
-import math
 
 import jax
 import jax.numpy as jnp
@@ -14,16 +13,6 @@
 BLK = 128
 MESH = pl.DeviceIdType.MESH
 
-R177 = math.sqrt(177.0)
-X3 = 2.0 / 3.0
-X1 = X3 * (1.0 + R177) / 88.0
-X2 = X3 * (1.0 + R177) / 352.0
-X4 = (-271.0 + 29.0 * R177) / (315.0 * X3)
-X5 = 11.0 * (-1.0 + R177) / (1260.0 * X3)
-X6 = 11.0 * (-9.0 + R177) / (5040.0 * X3)
-X7 = (89.0 - R177) / (5040.0 * X3 * X3)
-Y2 = (857.0 - 58.0 * R177) / 630.0
-
 
 def split(value):
     high = value.astype(jnp.bfloat16)
@@ -46,9 +35,9 @@
     dims, m_in, dp_in, gp_in, idx_in, tab_in,
     grad_ref, dir_ref, tfin, stat_ref,
     idx_ref, tab_ref, m_ref, gp_ref, dp_ref, in_s,
-    mall, dcm, drt, dsrc, gblk, blk2, blk4, eblk, etr, stile, sx, sz,
-    drow, dcol, grow, gcol, acol, row2, col2, row4, col4, erow, ej, mt, turned, part, pz, px, qtile, ttile,
-    a2a_s, a2a_r, dia_s, dia_r, dpr_s, dpr_r, row_s, row_r, col_s, col_r, fwd_s, fwd_r, one_s, one_r, sml_s, sml_r, pz_s, pz_r,
+    mall, dcm, drt, dsrc, gblk, blk1, blk2, blk3, blk4, eblk, etr, stile, sx, sz,
+    drow, dcol, grow, gcol, acol, row2, col2, row3, row4, col4, erow, ej, mt, turned, part, pz, px, qtile, ttile,
+    a2a_s, a2a_r, dia_s, dia_r, dpr_s, dpr_r, row_s, row_r, col_s, col_r, fwd_s, fwd_r, sml_s, sml_r, pz_s, pz_r,
 ):
     nx, ny, nz, nk = dims
     count = nx * ny
@@ -106,7 +95,6 @@
     for copy in loads:
         copy.wait()
 
-    mall[pl.ds(x, 1)] = m_ref[:, :, lanes(x)][None]
     own_d = dp_ref[:, lanes(x)]
     eye_r = lax.broadcasted_iota(jnp.int32, (BLK, BLK), 0)
     eye_c = lax.broadcasted_iota(jnp.int32, (BLK, BLK), 1)
@@ -116,8 +104,6 @@
         dsrc[p:p + 1, :] = jnp.sum(jnp.where(eye, m_ref[p, :, lanes(px_t)], 0.0), axis=0, keepdims=True)
     if nx * 8 < BLK:
         dcm[nx * 8:, :] = jnp.zeros((BLK - nx * 8, BLK), jnp.float32)
-    drow[:, lanes(y, wide)] = dp_ref[...]
-    dcol[lanes(r), :] = own_d
 
     expected = len(plane) + len(others)
     asked = len(line) - (x == px_t).astype(jnp.int32)
@@ -184,38 +170,66 @@
     ring_y = [1, ny - 1, 2]
 
     def plane_start(stage, src, dst):
+        bank = 1 if stage == 4 else 0
         first = []
         for i, ox in enumerate(ring_x):
-            first.append(remote(src, dst.at[:, lanes(c)], row_s.at[i], row_r.at[stage, i], at_plane(ox, 0)))
-            first.append(remote(src, dst.at[:, lanes(c)], row_s.at[3 + i], row_r.at[stage, 3 + i], at_plane(0, ring_y[i])))
-        for copy in first:
-            copy.start()
-        return stage, dst, first, []
+            for at, device in ((i, at_plane(ox, 0)), (3 + i, at_plane(0, ring_y[i]))):
+                first.append(remote(src, dst.at[:, lanes(c)], row_s.at[bank, at], row_r.at[stage, at], device))
+                first[-1].start()
+        return stage, bank, dst, first, []
 
     def plane_forward(state):
-        stage, dst, first, second = state
+        stage, bank, dst, first, second = state
         with jax.named_scope(f"row{stage}a"):
             for i in range(3):
                 first[2 * i].wait_recv()
                 held = dst.at[top, lanes(nx * y + off(x, nx - ring_x[i], nx))]
                 for j in range(3):
                     at = 6 + 3 * i + j
-                    second.append(remote(held, held, row_s.at[at], row_r.at[stage, at], at_plane(0, ring_y[j])))
+                    second.append(remote(held, held, row_s.at[bank, at], row_r.at[stage, at], at_plane(0, ring_y[j])))
                     second[-1].start()
                 first[2 * i + 1].wait_recv()
                 held = dst.at[low, lanes(nx * off(y, ny - ring_y[i], ny) + x)]
                 for j in range(3):
                     at = 15 + 3 * i + j
-                    second.append(remote(held, held, row_s.at[at], row_r.at[stage, at], at_plane(ring_x[j], 0)))
+                    second.append(remote(held, held, row_s.at[bank, at], row_r.at[stage, at], at_plane(ring_x[j], 0)))
                     second[-1].start()
 
+    arrivals = [(0, 0), (1, 0), (0, 1), (nx - 1, 0), (0, ny - 1), (2, 0), (0, 2)]
+    arrivals += [(ox, oy) for ox in (1, nx - 1) for oy in (1, ny - 1)]
+    arrivals += [(ox, oy) for ox, oy in plane if ox and oy and 2 in (ox, oy) and ox != oy] + [(2, 2)]
+    groups = [arrivals[i:i + 4] for i in range(0, len(arrivals), 4)]
+
+    def plane_pieces(state, pieces):
+        stage, _, _, first, second = state
+        with jax.named_scope(f"row{stage}w"):
+            for ox, oy in pieces:
+                if ox and oy:
+                    i, j = ring_x.index(ox), ring_y.index(oy)
+                    second[6 * i + j].wait_recv()
+                    second[6 * j + 3 + i].wait_recv()
+        return [lanes(nx * off(y, ny - oy if oy else 0, ny) + off(x, nx - ox if ox else 0, nx)) for ox, oy in pieces]
+
+    def plane_sum(state, left, right, acc, before_last=lambda: None):
+        for pieces in groups:
+            if pieces is groups[-1]:
+                before_last()
+            places = plane_pieces(state, pieces)
+            rows_l = jnp.concatenate([left[:, at] for at in places], axis=1)
+            cols_r = jnp.concatenate([right(at) for at in places], axis=0)
+            acc = acc + dot_split(split(rows_l), split(cols_r))
+        plane_done(state)
+        return acc
+
+    def plane_done(state):
+        _, _, _, first, second = state
+        for copy in first + second:
+            copy.wait_send()
+
     def plane_finish(state):
-        stage, _, first, second = state
-        with jax.named_scope(f"row{stage}b"):
-            for copy in second:
-                copy.wait()
-            for copy in first:
-                copy.wait_send()
+        for pieces in groups:
+            plane_pieces(state, pieces)
+        plane_done(state)
 
     def line_start(stage, src, slot):
         bank = 1 if stage == 0 else 0
@@ -253,9 +267,12 @@
                     first[oz].wait_recv()
                 line_across(state, oz)
 
-    def line_finish(state):
+    close = (0, 2, nz - 2, 1, nz - 1)
+    distant = (3, nz - 3, 4)
+
+    def line_far(state):
         stage, bank, slot, first, second, over = state
-        with jax.named_scope(f"line{stage}b"):
+        with jax.named_scope(f"line{stage}f"):
             second[0].wait_recv()
             line_across(state, 3)
             second[1].wait_recv()
@@ -263,10 +280,28 @@
             second[2].wait_recv()
             second[3].wait_recv()
             line_across(state, 4)
-            for copy in over:
-                copy.wait()
-            for copy in list(first.values()) + list(second.values()):
+
+    def line_mid(state):
+        with jax.named_scope(f"line{state[0]}m"):
+            for copy in state[5][:5]:
+                copy.wait_recv()
+
+    def line_done(state):
+        stage, bank, slot, first, second, over = state
+        with jax.named_scope(f"line{stage}d"):
+            for copy in over[5:]:
+                copy.wait_recv()
+            for copy in over + list(first.values()) + list(second.values()):
                 copy.wait_send()
+
+    def line_finish(state):
+        line_far(state)
+        line_mid(state)
+        line_done(state)
+
+    def part_of_sum(steps):
+        size = nk * BLK
+        return [pl.ds(pl.multiple_of(off(z, step, nz) * size, size), size) for step in steps]
 
     def column_slots(ref):
         def slot(index, part=slice(0, BLK)):
@@ -277,6 +312,11 @@
         return lambda index, part=slice(0, BLK): ref.at[part, lanes(index)]
 
     d_col = line_start(0, dp_ref.at[:, lanes(x)], column_slots(dcol))
+
+    mall[pl.ds(x, 1)] = m_ref[:, :, lanes(x)][None]
+    drow[:, lanes(y, wide)] = dp_ref[...]
+    dcol[lanes(r), :] = own_d
+    line_forward(d_col)
 
     for b in range(nx):
         @pl.when(jnp.logical_not(holds & (x == b)))
@@ -297,8 +337,14 @@
             value = value + jnp.where(idx_ref[b] == t, tab_ref[t], jnp.float32(0.0))
         weights.append(value)
 
+    row_index = lax.broadcasted_iota(jnp.int32, (nx, BLK), 0)
+    row_weights = []
+    for h in range(nk):
+        value = jnp.zeros((nx, BLK), jnp.float32)
+        for b in range(nx // nk):
+            value = jnp.where((row_index >= 2 * b) & (row_index < 2 * b + 2), weights[h * (nx // nk) + b], value)
+        row_weights.append(value)
     columns = jnp.transpose(dcm[...])
-    line_forward(d_col)
     line_near(d_col)
     far = []
     for i, (step, piece) in enumerate(((1, top), (ny - 1, low))):
@@ -320,12 +366,12 @@
     gblk[...] = total
     own_p = gp_ref[:, lanes(x)]
     first_line = (r == 0).astype(jnp.float32)
-    stile[...] = jnp.zeros((8, BLK), jnp.float32)
-    stile[0:1, :] = jnp.sum(total * total, axis=0, keepdims=True)
-    stile[1:2, :] = jnp.sum(total * own_d, axis=0, keepdims=True)
-    stile[2:3, :] = jnp.sum(own_d * own_d, axis=0, keepdims=True)
-    stile[3:4, :] = jnp.sum(own_p * own_p, axis=0, keepdims=True)
-    stile[4:5, :] = spread_row * first_line
+    sums = [total * total, total * own_d, own_d * own_d, own_p * own_p]
+    row_sums = [jnp.sum(value, axis=0, keepdims=True) for value in sums] + [spread_row * first_line]
+    row_sums.append(jnp.zeros((8 - len(row_sums), BLK), jnp.float32))
+    row_sums = jnp.sum(jnp.concatenate(row_sums, axis=0), axis=1, keepdims=True)
+    pick = lax.broadcasted_iota(jnp.int32, (8, BLK), 0) == lax.broadcasted_iota(jnp.int32, (8, BLK), 1)
+    stile[...] = jnp.sum(jnp.where(pick, row_sums, 0.0), axis=0, keepdims=True)
 
     def small_plane(stage, src, dst):
         dst[pl.ds(c, 1)] = src[...][None]
@@ -357,143 +403,179 @@
     gcol[lanes(r), :] = total
     rows = plane_start(0, gblk, grow)
     cols = line_start(1, gblk, column_slots(gcol))
+    wait_all(copies, "small0")
+    stile[...] = summed(sx)
+    copies = small_plane(1, stile, sz)
     line_forward(cols)
     plane_forward(rows)
     line_near(cols)
     line_finish(d_col)
-    wait_all(copies, "small0")
-    stile[...] = summed(sx)
-    copies = small_plane(1, stile, sz)
     wait_all(far, "far")
     for copy in dprow:
         copy.wait_send()
-    line_finish(cols)
+    line_far(cols)
     plane_finish(rows)
+    line_mid(cols)
     wait_all(copies, "small1")
-    sums = jnp.broadcast_to(jnp.sum(summed(sz), axis=1, keepdims=True), (8, BLK))
-    gg, gd, dd, pp = (sums[i:i + 1, :] for i in range(4))
-    spread = sums[4:5, :] / order
+    sums = jnp.sum(jnp.where(pick, summed(sz), 0.0), axis=1, keepdims=True)
+    gg, gd, dd, pp, spread = (jnp.broadcast_to(sums[i:i + 1, :], (1, BLK)) for i in range(5))
+    spread = spread / order
     beta = gg / (1.0 + pp)
     norm = jnp.maximum(gg - 2.0 * beta * gd + beta * beta * dd, 0.0)
     scale = STEP_SCALE / jnp.sqrt(1.0 + norm / order)
 
+    chunk = 4 * BLK if order % (4 * BLK) == 0 else BLK
+    beta_w = jnp.concatenate([beta] * nk, axis=1)
+    scale_w = jnp.concatenate([scale] * nk, axis=1)
+
+    def square(acc, steps):
+        for at in part_of_sum(steps):
+            left = scale_w * (beta_w * drow[:, at] - grow[:, at])
+            right = scale * (beta * dcol[at, :] - gcol[at, :])
+            acol[at, :] = right
+            acc = acc + dot_split(split(left), split(right))
+        return acc
+
+    acc = square(jnp.zeros((BLK, BLK), jnp.float32), close)
+    line_done(cols)
+    acc = square(acc, distant)
+    blk1[...] = acol[lanes(r), :]
+    blk2[...] = acc
+    row2[:, lanes(c)] = acc
+    col2[lanes(r), :] = acc
+    rows = plane_start(1, blk2, row2)
+    cols = line_start(2, blk2, column_slots(col2))
     for j in range(nx):
         at = pl.ds(pl.multiple_of(y * wide + j * BLK, BLK), BLK)
         piece = grow[:, at]
         grad_ref[:, j * BLK:(j + 1) * BLK] = piece
         dir_ref[:, j * BLK:(j + 1) * BLK] = beta * drow[:, at] - piece
 
-    chunk = 4 * BLK if order % (4 * BLK) == 0 else BLK
-    beta_w = jnp.concatenate([beta] * (chunk // BLK), axis=1)
-    scale_w = jnp.concatenate([scale] * (chunk // BLK), axis=1)
-
-    acc = jnp.zeros((BLK, BLK), jnp.float32)
-    for at in range(0, order, chunk):
-        left = scale_w * (beta_w * drow[:, at:at + chunk] - grow[:, at:at + chunk])
-        right = scale * (beta * dcol[at:at + chunk, :] - gcol[at:at + chunk, :])
-        acol[at:at + chunk, :] = right
-        acc = acc + dot_split(split(left), split(right))
-    blk2[...] = acc
-    row2[:, lanes(c)] = acc
-    col2[lanes(r), :] = acc
-    rows = plane_start(1, blk2, row2)
-    cols = line_start(2, blk2, column_slots(col2))
     for b in range(nx):
         for p in range(2):
             i = 2 * b + p
             high, tail = split(jnp.transpose(mall[b, p]))
-            mt[i * BLK:(i + 1) * BLK, :] = jnp.concatenate([high, tail], axis=1)
+            mt[i * BLK:(i + 1) * BLK, :] = jnp.concatenate([high, tail, high], axis=1)
     line_forward(cols)
     plane_forward(rows)
     line_near(cols)
+    acc3 = plane_sum(
+        rows, row2, lambda at: acol[at, :], jnp.zeros((BLK, BLK), jnp.float32), lambda: line_far(cols)
+    )
+    blk3[...] = acc3
+    row3[:, lanes(c)] = acc3
+    more = plane_start(4, blk3, row3)
+    line_mid(cols)
+
+    def fourth(acc, steps):
+        for at in part_of_sum(steps):
+            acc = acc + dot_split(split(row2[:, at]), split(col2[at, :]))
+        return acc
+
+    acc4 = fourth(jnp.zeros((BLK, BLK), jnp.float32), close)
+    line_done(cols)
+    acc4 = fourth(acc4, distant)
+    blk4[...] = acc4
+    row4[:, lanes(c)] = acc4
+    col4[lanes(r), :] = acc4
+    cols = line_start(3, blk4, column_slots(col4))
+    rows = plane_start(2, blk4, row4)
+    plane_forward(more)
+    for at in range(0, order, chunk):
+        acol[at:at + chunk, :] = col2[at:at + chunk, :] * (1.0 / 720.0)
+        gcol[at:at + chunk, :] = col2[at:at + chunk, :] * (1.0 / 120.0)
+    line_forward(cols)
+    line_near(cols)
+    plane_forward(rows)
     line_finish(cols)
-    plane_finish(rows)
-
-    acc = jnp.zeros((BLK, BLK), jnp.float32)
+    plane_finish(more)
+
+    odd = jnp.zeros((BLK, BLK), jnp.float32)
     for at in range(0, order, chunk):
-        right = X1 * acol[at:at + chunk, :] + X2 * col2[at:at + chunk, :]
-        acc = acc + dot_split(split(row2[:, at:at + chunk]), split(right))
-    blk4[...] = acc
-    row4[:, lanes(c)] = acc
-    col4[lanes(r), :] = acc
-    rows = plane_start(2, blk4, row4)
-    cols = line_start(3, blk4, column_slots(col4))
-    for at in range(0, order, chunk):
-        grow[:, at:at + chunk] = X3 * row2[:, at:at + chunk]
-        gcol[at:at + chunk, :] = X5 * acol[at:at + chunk, :] + X6 * col2[at:at + chunk, :]
-    line_forward(cols)
-    plane_forward(rows)
-    line_near(cols)
-    line_finish(cols)
-    plane_finish(rows)
-
-    acc = jnp.zeros((BLK, BLK), jnp.float32)
-    for at in range(0, order, chunk):
-        left = grow[:, at:at + chunk] + row4[:, at:at + chunk]
-        right = gcol[at:at + chunk, :] + X7 * col4[at:at + chunk, :]
-        acc = acc + dot_split(split(left), split(right))
-    acc = acc + X4 * (X3 * blk2[...] + blk4[...]) + Y2 * blk2[...] + acol[lanes(r), :]
-    acc = acc + jnp.where(eye & jnp.logical_not(off_diag), 1.0, 0.0)
-    eblk[...] = acc
-
-    turn = remote(eblk, etr, one_s.at[0], one_r.at[0], dev(px_t, py_t, pz_t, pk_t))
-
-    @pl.when(off_diag)
-    def _():
-        turn.start()
-
-    erow[:, lanes(c)] = acc
+        right = gcol[at:at + chunk, :] + col4[at:at + chunk, :] * (1.0 / 5040.0)
+        odd = odd + dot_split(split(row3[:, at:at + chunk]), split(right))
+    odd = odd + blk1[...] + blk3[...] * (1.0 / 6.0)
+    def even_columns(at):
+        return acol[at, :] + col4[at, :] * (1.0 / 40320.0)
+
+    even = plane_sum(rows, row4, even_columns, jnp.zeros((BLK, BLK), jnp.float32))
+    even = even + blk2[...] * 0.5 + blk4[...] * (1.0 / 24.0)
+    even = even + jnp.where(eye & jnp.logical_not(off_diag), 1.0, 0.0)
+
+    eblk[...] = even + odd
+    etr[...] = jnp.transpose(even - odd)
+    cols = line_start(4, etr, row_slots(ej))
     rows = plane_start(3, eblk, erow)
-
-    @pl.when(off_diag)
-    def _():
-        with jax.named_scope("turn"):
-            turn.wait()
-
-    @pl.when(jnp.logical_not(off_diag))
-    def _():
-        etr[...] = eblk[...]
-
-    cols = line_start(4, etr, row_slots(ej))
+    erow[:, lanes(c)] = eblk[...]
     ej[:, lanes(r)] = etr[...]
     plane_forward(rows)
     line_forward(cols)
     line_near(cols)
-    plane_finish(rows)
-    for at in range(0, order, chunk):
-        high, tail = split(erow[:, at:at + chunk])
-        turned[:, at:at + chunk] = dot(mt[...], jnp.concatenate([high, high], axis=0)) + dot(mt[:, :BLK], tail)
-    line_finish(cols)
-
-    def to_owner(j):
-        return remote(part.at[:, j * BLK:(j + 1) * BLK], pz.at[r], pz_s.at[j], pz_r.at[r], dev(x, y, j // nk, j % nk))
-
-    for at in range(0, order, chunk):
-        left = ej[:, at:at + chunk]
-        for i in range(2 * nx):
-            part[i:i + 1, at:at + chunk] = jnp.sum(
-                left * turned[i * BLK:(i + 1) * BLK, at:at + chunk], axis=0, keepdims=True
+
+    def turn(g):
+        slots = plane_pieces(rows, groups[g])
+        high, tail = split(jnp.concatenate([erow[:, at] for at in slots], axis=1))
+        turned[g] = dot(mt[...], jnp.concatenate([high, high, tail], axis=0))
+
+    for g in range(len(groups) - 1):
+        turn(g)
+    line_far(cols)
+    turn(len(groups) - 1)
+    plane_done(rows)
+
+    hall = [(ox, oy, ok) for ox in range(nx) for oy in range(ny) for ok in range(nk)]
+
+    def at_hall(ox, oy, ok):
+        return dev(off(x, ox, nx), off(y, oy, ny), z, off(k, ok, nk))
+
+    line_mid(cols)
+    line_done(cols)
+    own = nk * c + k
+    copies = []
+    for g, pieces in enumerate(groups):
+        for i, (ox, oy) in enumerate(pieces):
+            back = (nx - ox) % nx, (ny - oy) % ny
+            place = nx * off(y, back[1], ny) + off(x, back[0], nx)
+            left = ej[:, lanes(place)]
+            sums = jnp.concatenate(
+                [
+                    jnp.sum(left * turned[g, j * BLK:(j + 1) * BLK, i * BLK:(i + 1) * BLK], axis=0, keepdims=True)
+                    for j in range(2 * nx)
+                ],
+                axis=0,
             )
-        for j in range(at // BLK, (at + chunk) // BLK):
-            @pl.when(r != j)
-            def _(j=j):
-                to_owner(j).start()
-
-    pz[pl.ds(r, 1)] = part[:, lanes(r)][None]
-    with jax.named_scope("small2"):
-        for oz, ok in others:
-            rp = nk * off(z, oz, nz) + off(k, ok, nk)
-            remote(pz.at[rp], pz.at[rp], pz_s.at[0], pz_r.at[rp], at_line(oz, ok)).wait_recv()
-    qtile[...] = summed(pz)
-    wait_all(small_plane(3, qtile, px), "small3")
-    sumt = summed(px)
-    ttile[...] = sumt
-    tfin[:, lanes(r)] = sumt
+            for h in range(nk):
+                part[nk * (4 * g + i) + h] = sums[h * nx:(h + 1) * nx]
+        for i, (ox, oy) in enumerate(pieces):
+            back = (nx - ox) % nx, (ny - oy) % ny
+            for ok in range(nk):
+                src = part.at[nk * (4 * g + i) + off(k, ok, nk)]
+                if (ox, oy, ok) == (0, 0, 0):
+                    pz[pl.ds(own, 1)] = part[pl.ds(nk * (4 * g + i) + k, 1)]
+                else:
+                    at = hall.index((*back, ok))
+                    copies.append(remote(src, pz.at[own], pz_s.at[at], pz_r.at[0, at], at_hall(*back, ok)))
+                    copies[-1].start()
+    wait_all(copies, "small2")
+    value = pz[0]
+    for i in range(1, nk * count):
+        value = value + pz[i]
+    ttile[...] = value
+    px[pl.ds(z, 1)] = value[None]
     copies = []
-    for i, (oz, ok) in enumerate(others):
-        copy = remote(ttile, tfin.at[:, lanes(r)], sml_s.at[i], sml_r.at[4, i], at_line(oz, ok))
-        copy.start()
-        copies.append(copy)
+    for oz in range(1, nz):
+        copies.append(remote(ttile, px.at[z], pz_s.at[oz], pz_r.at[1, oz], at_line(oz, 0)))
+        copies[-1].start()
+    wait_all(copies, "small3")
+    value = px[0]
+    for i in range(1, nz):
+        value = value + px[i]
+    qtile[...] = value
+    tfin[pl.ds(own, 1)] = value[None]
+    copies = []
+    for i, (ox, oy, ok) in enumerate(hall[1:]):
+        copies.append(remote(qtile, tfin.at[own], pz_s.at[i], pz_r.at[2, i], at_hall(ox, oy, ok)))
+        copies[-1].start()
 
     @pl.when(holds)
     def _():
@@ -506,16 +588,14 @@
     def _():
         dia_col[0].wait_send()
 
-    for j in range(count):
-        @pl.when(r != j)
-        def _(j=j):
-            to_owner(j).wait_send()
-
     wait_all(copies, "small4")
-    trial = jnp.zeros((1, order), jnp.float32)
-    for b in range(nx):
-        re_t, im_t = tfin[2 * b:2 * b + 1, :], tfin[2 * b + 1:2 * b + 2, :]
-        trial = trial + weights[b] * (1.0 - re_t * re_t - im_t * im_t)
+    trial = jnp.zeros((nx, BLK), jnp.float32)
+    for h in range(nk):
+        value = jnp.zeros((nx, BLK), jnp.float32)
+        for i in range(count):
+            value = value + (0.5 - tfin[nk * i + h] * tfin[nk * i + h])
+        trial = trial + value * row_weights[h]
+    trial = jnp.sum(trial, axis=0, keepdims=True)
     stat_ref[...] = jnp.zeros((8, BLK), jnp.float32)
     stat_ref[0:1, :] = spread
     stat_ref[1:2, :] = jnp.broadcast_to(jnp.sum(trial, axis=1, keepdims=True) / order, (1, BLK))
@@ -526,8 +606,11 @@
     trial_spread_out[0, 0] = jnp.sum(stat_ref[1:2, 0:1])
     grad_out[...] = grad_ref[...]
     dir_out[...] = dir_ref[...]
-    for b in range(trial_out.shape[0]):
-        trial_out[b] = trial_ref[2 * b:2 * b + 2, :]
+    halves = trial_out.shape[0] // 2
+    for i in range(trial_ref.shape[0] // 2):
+        for b in range(trial_out.shape[0]):
+            at = 2 * (b % halves)
+            trial_out[b, :, i * BLK:(i + 1) * BLK] = trial_ref[2 * i + b // halves, at:at + 2, :]
 
 
 def shards(dims, m_matrices, bvec_index, weight_table, grad_prev, dir_prev):
@@ -542,7 +625,9 @@
     tall = pltpu.VMEM((order, BLK), f32)
     block = pltpu.VMEM((BLK, BLK), f32)
     tile = pltpu.VMEM((8, BLK), f32)
-    tiles = pltpu.VMEM((count, 8, BLK), f32)
+    half_tile = pltpu.VMEM((nx, BLK), f32)
+    line = pltpu.VMEM((1, BLK), f32)
+    lines = pltpu.VMEM((count, 1, BLK), f32)
     dma = pltpu.SemaphoreType.DMA
     n_plane, n_line = count - 1, nz * nk
     grad, direction, trial, stat = pl.pallas_call(
@@ -550,7 +635,7 @@
         out_shape=(
             jax.ShapeDtypeStruct((rows, cols), f32),
             jax.ShapeDtypeStruct((rows, cols), f32),
-            jax.ShapeDtypeStruct((8, order), f32),
+            jax.ShapeDtypeStruct((nk * count, nx, BLK), f32),
             jax.ShapeDtypeStruct((8, BLK), f32),
         ),
         in_specs=[pl.BlockSpec(memory_space=pltpu.HBM)] * 5,
@@ -559,18 +644,18 @@
             pltpu.SMEM(bvec_index.shape, jnp.int32), pltpu.SMEM(weight_table.shape, f32),
             pltpu.VMEM(m_matrices.shape[1:], f32), pltpu.VMEM((rows, cols), f32), pltpu.VMEM((rows, cols), f32), dma((5,)),
             pltpu.VMEM((nx, 2, BLK, BLK), f32), block, pltpu.VMEM((nx, 8, BLK), f32), tile,
-            block, block, block, block, block, tile, tiles, tiles,
-            wide, tall, wide, tall, tall, wide, tall, wide, tall, wide, wide,
-            pltpu.VMEM((2 * nx * BLK, 2 * BLK), jnp.bfloat16), pltpu.VMEM((2 * nx * BLK, order), f32),
-            pltpu.VMEM((8, order), f32), tiles, tiles, tile, tile,
+            block, block, block, block, block, block, block, line, lines, lines,
+            wide, tall, wide, tall, tall, wide, tall, wide, wide, tall, wide, wide,
+            pltpu.VMEM((2 * nx * BLK, 3 * BLK), jnp.bfloat16), pltpu.VMEM((count // 4, 2 * nx * BLK, 4 * BLK), f32),
+            pltpu.VMEM((nk * count, nx, BLK), f32), pltpu.VMEM((nk * count, nx, BLK), f32), pltpu.VMEM((nz, nx, BLK), f32),
+            half_tile, half_tile,
             dma((nx - 1,)), dma((nx - 1,)),
             dma((n_plane + n_line,)), dma((2 * nx,)),
             dma((4,)), dma((4,)),
-            dma((24,)), dma((4, 24)),
+            dma((2, 24)), dma((5, 24)),
             dma((2, 8)), dma((5, 8)),
             dma((2, nz)), dma((5, nz)),
-            dma((1,)), dma((1,)),
-            dma((n_plane,)), dma((5, n_plane)), dma((count,)), dma((count,)),
+            dma((n_plane,)), dma((2, n_plane)), dma((nk * count,)), dma((3, nk * count)),
         ],
         compiler_params=pltpu.CompilerParams(
             collective_id=0, has_side_effects=True, vmem_limit_bytes=40 * 1024 * 1024

time: 102 us -> 96.8 us (0.949)
  Pallas kernels: 101 us -> 96 us
    pallas_call x1, Pallas kernels: 101 us -> 95.2 us  [shards(): pl.pallas_call(functools.partial(kernel, dims), out_shape=(jax.ShapeDtype...]
where the time goes in v4:
time: 96.8 us; the launch traced here: 96.7 us
  Pallas kernels  96 us (99%)
    pallas_call x1, Pallas kernels, shards(): pl.pallas_call(functools.partial(kernel, dims), out_shape=(jax.ShapeDtype...  95.2 us

profile of v4, /device:TPU:1, one launch (start us, length us, event | category | flops | bytes accessed | tf_op | source)
XLA Modules:
  0.0 96.7 jit_solution(16282782532429210768)
XLA Ops:
  0.6 95.2 %shard_map.92 = (f32[128,512]{1,0:T(8,128)S(1)}, f32[128,512]{1,0:T(8,128)S(1)}, f32[32,4,128]{2,1,0:T(4,128)S(1)}, f32[8,128]{1,0:T(8,128)S(1)}) custom-call(f32[2,128,512]{2,1,0:T(8,128)} %bitcast.3, f32[128,512]{1,0:T(8,128)} %dp_in.1, f32[128,512]{1,0:T(8,128)} %gp_in.1, s32[4]{0:T(128)} %idx_in.1, f32[6]{0:T(128)} %tab_in.1), custom_call_target="tpu_custom_call" | custom-call | tf_op jit(solution)/shard_map/pallas_call | solution.py:633
  95.8 0.8 shard_map.93

commit v5 on v4

--- a/solution.py
+++ b/solution.py
@@ -35,9 +35,9 @@
     dims, m_in, dp_in, gp_in, idx_in, tab_in,
     grad_ref, dir_ref, tfin, stat_ref,
     idx_ref, tab_ref, m_ref, gp_ref, dp_ref, in_s,
-    mall, dcm, drt, dsrc, gblk, blk1, blk2, blk3, blk4, eblk, etr, stile, sx, sz,
+    mall, dcm, drt, dsrc, gblk, blk1, blk2, blk3, blk4, eblk, etr, own_block, stile, sx, sz,
     drow, dcol, grow, gcol, acol, row2, col2, row3, row4, col4, erow, ej, mt, turned, part, pz, px, qtile, ttile,
-    a2a_s, a2a_r, dia_s, dia_r, dpr_s, dpr_r, row_s, row_r, col_s, col_r, fwd_s, fwd_r, sml_s, sml_r, pz_s, pz_r,
+    a2a_s, a2a_r, dia_s, dia_r, dpr_s, dpr_r, row_s, row_r, col_s, col_r, fwd_s, fwd_r, sml_s, sml_r,
 ):
     nx, ny, nz, nk = dims
     count = nx * ny
@@ -115,12 +115,21 @@
             src_ref=src, dst_ref=dst, send_sem=send, recv_sem=recv, device_id=device, device_id_type=MESH
         )
 
+    def all_sent(sem, ref):
+        remote(ref, ref, sem, sem, dev(x, y, z, k)).wait_send()
+
+    def all_here(sem, ref):
+        remote(ref, ref, sem, sem, dev(x, y, z, k)).wait_recv()
+
+    def pieces_of(count_blocks):
+        return gcol.at[0:int(count_blocks * BLK), :]
+
     dia_row = [
-        remote(dsrc, dcm.at[pl.ds(pl.multiple_of(8 * x, 8), 8), :], dia_s.at[i], dia_r.at[x], at_plane(ox, oy))
+        remote(dsrc, dcm.at[pl.ds(pl.multiple_of(8 * x, 8), 8), :], dia_s.at[0], dia_r.at[x], at_plane(ox, oy))
         for i, (ox, oy) in enumerate(plane)
     ]
     dia_col = [
-        remote(dsrc, drt.at[x], dia_s.at[len(plane) + i], dia_r.at[nx + x],
+        remote(dsrc, drt.at[x], dia_s.at[0], dia_r.at[nx + x],
                dev(px_t, y, off(z, oz, nz), off(k, ok, nk)))
         for i, (oz, ok) in enumerate(line)
     ]
@@ -144,7 +153,7 @@
     a2a = []
     for ox in range(1, nx):
         xp = off(x, ox, nx)
-        copy = remote(m_ref.at[:, :, lanes(xp)], mall.at[x], a2a_s.at[ox - 1], a2a_r.at[ox - 1], dev(xp, y, z, k))
+        copy = remote(m_ref.at[:, :, lanes(xp)], mall.at[x], a2a_s.at[0], a2a_r.at[0], dev(xp, y, z, k))
         copy.start()
         a2a.append(copy)
 
@@ -158,24 +167,35 @@
 
     def far_block(step, part, index):
         held = drow.at[part, lanes(off(y, ny - step, ny), wide)]
-        return remote(held, held, dpr_s.at[index], dpr_r.at[index], at_plane(0, step))
+        return remote(held, held, dpr_s.at[0], dpr_r.at[index], at_plane(0, step))
 
     dprow = []
     for i, oy in enumerate((1, ny - 1)):
-        copy = remote(dp_ref, drow.at[:, lanes(y, wide)], dpr_s.at[i], dpr_r.at[i], at_plane(0, oy))
+        copy = remote(dp_ref, drow.at[:, lanes(y, wide)], dpr_s.at[0], dpr_r.at[i], at_plane(0, oy))
         copy.start()
         dprow.append(copy)
 
     ring_x = [1, nx - 1, 2]
     ring_y = [1, ny - 1, 2]
 
+    arrivals = [(0, 0), (1, 0), (0, 1), (nx - 1, 0), (0, ny - 1), (2, 0), (0, 2)]
+    arrivals += [(ox, oy) for ox in (1, nx - 1) for oy in (1, ny - 1)]
+    arrivals += [(ox, oy) for ox, oy in plane if ox and oy and 2 in (ox, oy) and ox != oy] + [(2, 2)]
+    groups = [arrivals[i:i + 4] for i in range(0, len(arrivals), 4)]
+
+    def group_sem(bank, ox, oy):
+        return row_r.at[bank, 6 + [g for g, pieces in enumerate(groups) if (ox, oy) in pieces][0]]
+
     def plane_start(stage, src, dst):
-        bank = 1 if stage == 4 else 0
+        bank = 2 if stage == 4 else stage % 2
         first = []
-        for i, ox in enumerate(ring_x):
-            for at, device in ((i, at_plane(ox, 0)), (3 + i, at_plane(0, ring_y[i]))):
-                first.append(remote(src, dst.at[:, lanes(c)], row_s.at[bank, at], row_r.at[stage, at], device))
-                first[-1].start()
+        for n, (over_x, over_y) in enumerate(((top, low), (low, top))):
+            for i in range(3):
+                for m, part_of, device in ((0, over_x, at_plane(ring_x[i], 0)), (1, over_y, at_plane(0, ring_y[i]))):
+                    step = (0, ring_y[i]) if m else (ring_x[i], 0)
+                    sem = group_sem(bank, *step) if n else row_r.at[bank, 2 * i + m]
+                    first.append(remote(src.at[part_of, :], dst.at[part_of, lanes(c)], row_s.at[bank], sem, device))
+                    first[-1].start()
         return stage, bank, dst, first, []
 
     def plane_forward(state):
@@ -185,29 +205,21 @@
                 first[2 * i].wait_recv()
                 held = dst.at[top, lanes(nx * y + off(x, nx - ring_x[i], nx))]
                 for j in range(3):
-                    at = 6 + 3 * i + j
-                    second.append(remote(held, held, row_s.at[bank, at], row_r.at[stage, at], at_plane(0, ring_y[j])))
+                    sem = group_sem(bank, ring_x[i], ring_y[j])
+                    second.append(remote(held, held, row_s.at[bank], sem, at_plane(0, ring_y[j])))
                     second[-1].start()
                 first[2 * i + 1].wait_recv()
                 held = dst.at[low, lanes(nx * off(y, ny - ring_y[i], ny) + x)]
                 for j in range(3):
-                    at = 15 + 3 * i + j
-                    second.append(remote(held, held, row_s.at[bank, at], row_r.at[stage, at], at_plane(ring_x[j], 0)))
+                    sem = group_sem(bank, ring_x[j], ring_y[i])
+                    second.append(remote(held, held, row_s.at[bank], sem, at_plane(ring_x[j], 0)))
                     second[-1].start()
 
-    arrivals = [(0, 0), (1, 0), (0, 1), (nx - 1, 0), (0, ny - 1), (2, 0), (0, 2)]
-    arrivals += [(ox, oy) for ox in (1, nx - 1) for oy in (1, ny - 1)]
-    arrivals += [(ox, oy) for ox, oy in plane if ox and oy and 2 in (ox, oy) and ox != oy] + [(2, 2)]
-    groups = [arrivals[i:i + 4] for i in range(0, len(arrivals), 4)]
-
     def plane_pieces(state, pieces):
-        stage, _, _, first, second = state
+        stage, bank, _, _, _ = state
+        halves = sum(2 if ox and oy else 1 for ox, oy in pieces if (ox, oy) != (0, 0))
         with jax.named_scope(f"row{stage}w"):
-            for ox, oy in pieces:
-                if ox and oy:
-                    i, j = ring_x.index(ox), ring_y.index(oy)
-                    second[6 * i + j].wait_recv()
-                    second[6 * j + 3 + i].wait_recv()
+            all_here(row_r.at[bank, 6 + groups.index(pieces)], pieces_of(halves / 2))
         return [lanes(nx * off(y, ny - oy if oy else 0, ny) + off(x, nx - ox if ox else 0, nx)) for ox, oy in pieces]
 
     def plane_sum(state, left, right, acc, before_last=lambda: None):
@@ -222,9 +234,7 @@
         return acc
 
     def plane_done(state):
-        _, _, _, first, second = state
-        for copy in first + second:
-            copy.wait_send()
+        all_sent(row_s.at[state[1]], pieces_of(count - 1))
 
     def plane_finish(state):
         for pieces in groups:
@@ -232,39 +242,42 @@
         plane_done(state)
 
     def line_start(stage, src, slot):
-        bank = 1 if stage == 0 else 0
+        bank = (2, 0, 1, 0, 1)[stage]
+        whole = slice(0, BLK)
         first = {}
-        for i, oz in enumerate((2, nz - 2, 1, nz - 1)):
-            first[oz] = remote(src, slot(r), col_s.at[bank, i], col_r.at[stage, i], at_line(oz, 0))
-            first[oz].start()
-        over = [remote(src, slot(r), fwd_s.at[bank, 0], fwd_r.at[stage, 0], at_line(0, 1))]
+        order_z = ((2, top), (nz - 2, low), (2, low), (nz - 2, top), (1, whole), (nz - 1, whole))
+        for i, (oz, piece) in enumerate(order_z):
+            first[oz, piece.start] = remote(
+                src.at[piece, :], slot(r, piece), col_s.at[bank], col_r.at[bank, i], at_line(oz, 0)
+            )
+            first[oz, piece.start].start()
+        over = [remote(src, slot(r), fwd_s.at[bank], fwd_r.at[bank, 0], at_line(0, 1))]
         over[0].start()
         return stage, bank, slot, first, {}, over
 
     def line_across(state, oz):
         stage, bank, slot, first, second, over = state
         held = slot(nk * off(z, nz - oz, nz) + k)
-        over.append(remote(held, held, fwd_s.at[bank, oz], fwd_r.at[stage, oz], at_line(0, 1)))
+        over.append(remote(held, held, fwd_s.at[bank], fwd_r.at[bank, 1 if oz in distant else 0], at_line(0, 1)))
         over[-1].start()
 
     def line_forward(state):
         stage, bank, slot, first, second, over = state
         with jax.named_scope(f"line{stage}a"):
-            for i, (oz, step, part) in enumerate(((2, 1, top), (nz - 2, nz - 1, low))):
-                first[oz].wait_recv()
-                held = slot(nk * off(z, nz - oz, nz) + k)
-                second[i] = remote(held, held, col_s.at[bank, 4 + i], col_r.at[stage, 4 + i], at_line(step, 0))
-                second[i].start()
-                held = slot(nk * off(z, nz - oz, nz) + k, part)
-                second[2 + i] = remote(held, held, col_s.at[bank, 6 + i], col_r.at[stage, 6 + i], at_line(oz, 0))
-                second[2 + i].start()
+            steps = ((2, top, (2, 1)), (nz - 2, low, (nz - 2, nz - 1)), (2, low, (1,)), (nz - 2, top, (nz - 1,)))
+            for oz, piece, onward in steps:
+                first[oz, piece.start].wait_recv()
+                held = slot(nk * off(z, nz - oz, nz) + k, piece)
+                for step in onward:
+                    at = 6 + distant.index((oz + step) % nz)
+                    remote(held, held, col_s.at[bank], col_r.at[bank, at], at_line(step, 0)).start()
 
     def line_near(state):
         stage, bank, slot, first, second, over = state
         with jax.named_scope(f"line{stage}n"):
             for oz in (2, nz - 2, 1, nz - 1):
                 if oz in (1, nz - 1):
-                    first[oz].wait_recv()
+                    first[oz, 0].wait_recv()
                 line_across(state, oz)
 
     close = (0, 2, nz - 2, 1, nz - 1)
@@ -273,26 +286,20 @@
     def line_far(state):
         stage, bank, slot, first, second, over = state
         with jax.named_scope(f"line{stage}f"):
-            second[0].wait_recv()
-            line_across(state, 3)
-            second[1].wait_recv()
-            line_across(state, nz - 3)
-            second[2].wait_recv()
-            second[3].wait_recv()
-            line_across(state, 4)
+            for oz in (3, nz - 3, 4):
+                all_here(col_r.at[bank, 6 + distant.index(oz)], pieces_of(1))
+                line_across(state, oz)
 
     def line_mid(state):
         with jax.named_scope(f"line{state[0]}m"):
-            for copy in state[5][:5]:
-                copy.wait_recv()
+            all_here(fwd_r.at[state[1], 0], pieces_of(len(close)))
 
     def line_done(state):
         stage, bank, slot, first, second, over = state
         with jax.named_scope(f"line{stage}d"):
-            for copy in over[5:]:
-                copy.wait_recv()
-            for copy in over + list(first.values()) + list(second.values()):
-                copy.wait_send()
+            all_here(fwd_r.at[bank, 1], pieces_of(len(distant)))
+            all_sent(fwd_s.at[bank], pieces_of(nz))
+            all_sent(col_s.at[bank], pieces_of(nz - 1))
 
     def line_finish(state):
         line_far(state)
@@ -311,7 +318,8 @@
     def row_slots(ref):
         return lambda index, part=slice(0, BLK): ref.at[part, lanes(index)]
 
-    d_col = line_start(0, dp_ref.at[:, lanes(x)], column_slots(dcol))
+    own_block[...] = own_d
+    d_col = line_start(0, own_block, column_slots(dcol))
 
     mall[pl.ds(x, 1)] = m_ref[:, :, lanes(x)][None]
     drow[:, lanes(y, wide)] = dp_ref[...]
@@ -351,7 +359,8 @@
         dprow[i].wait_recv()
         far.append(far_block(step, piece, 2 + i))
         far[-1].start()
-    wait_all(a2a, "a2a")
+    with jax.named_scope("a2a"):
+        all_here(a2a_r.at[0], mall.at[0:nx - 1])
     total = jnp.zeros((BLK, BLK), jnp.float32)
     spread_row = jnp.zeros((1, BLK), jnp.float32)
     for b in range(nx):
@@ -377,7 +386,7 @@
         dst[pl.ds(c, 1)] = src[...][None]
         copies = []
         for i, (ox, oy) in enumerate(plane):
-            copy = remote(src, dst.at[c], sml_s.at[i], sml_r.at[stage, i], at_plane(ox, oy))
+            copy = remote(src, dst.at[c], sml_s.at[stage], sml_r.at[stage], at_plane(ox, oy))
             copy.start()
             copies.append(copy)
         return copies
@@ -387,7 +396,7 @@
         copies = []
         for i, (oz, ok) in enumerate(others):
             rp = nk * off(z, oz, nz) + off(k, ok, nk)
-            copy = remote(src(rp), dst.at[r], sml_s.at[i], sml_r.at[stage, i], at_line(oz, ok))
+            copy = remote(src(rp), dst.at[r], sml_s.at[stage], sml_r.at[stage], at_line(oz, ok))
             copy.start()
             copies.append(copy)
         return copies
@@ -403,20 +412,26 @@
     gcol[lanes(r), :] = total
     rows = plane_start(0, gblk, grow)
     cols = line_start(1, gblk, column_slots(gcol))
-    wait_all(copies, "small0")
+    with jax.named_scope("small0"):
+        all_here(sml_r.at[0], sx.at[0:count - 1])
+    all_sent(sml_s.at[0], sx.at[0:count - 1])
     stile[...] = summed(sx)
     copies = small_plane(1, stile, sz)
     line_forward(cols)
     plane_forward(rows)
     line_near(cols)
     line_finish(d_col)
-    wait_all(far, "far")
-    for copy in dprow:
-        copy.wait_send()
+    with jax.named_scope("far"):
+        for copy in far:
+            copy.wait_recv()
+    all_sent(dpr_s.at[0], pieces_of(order // BLK * 3 / 4))
+    all_sent(a2a_s.at[0], mall.at[0:nx - 1])
     line_far(cols)
     plane_finish(rows)
     line_mid(cols)
-    wait_all(copies, "small1")
+    with jax.named_scope("small1"):
+        all_here(sml_r.at[1], sz.at[0:count - 1])
+    all_sent(sml_s.at[1], sz.at[0:count - 1])
     sums = jnp.sum(jnp.where(pick, summed(sz), 0.0), axis=1, keepdims=True)
     gg, gd, dd, pp, spread = (jnp.broadcast_to(sums[i:i + 1, :], (1, BLK)) for i in range(5))
     spread = spread / order
@@ -554,9 +569,11 @@
                     pz[pl.ds(own, 1)] = part[pl.ds(nk * (4 * g + i) + k, 1)]
                 else:
                     at = hall.index((*back, ok))
-                    copies.append(remote(src, pz.at[own], pz_s.at[at], pz_r.at[0, at], at_hall(*back, ok)))
+                    copies.append(remote(src, pz.at[own], sml_s.at[2], sml_r.at[2], at_hall(*back, ok)))
                     copies[-1].start()
-    wait_all(copies, "small2")
+    with jax.named_scope("small2"):
+        all_here(sml_r.at[2], pz.at[0:nk * count - 1])
+    all_sent(sml_s.at[2], pz.at[0:nk * count - 1])
     value = pz[0]
     for i in range(1, nk * count):
         value = value + pz[i]
@@ -564,9 +581,11 @@
     px[pl.ds(z, 1)] = value[None]
     copies = []
     for oz in range(1, nz):
-        copies.append(remote(ttile, px.at[z], pz_s.at[oz], pz_r.at[1, oz], at_line(oz, 0)))
+        copies.append(remote(ttile, px.at[z], sml_s.at[3], sml_r.at[3], at_line(oz, 0)))
         copies[-1].start()
-    wait_all(copies, "small3")
+    with jax.named_scope("small3"):
+        all_here(sml_r.at[3], px.at[0:nz - 1])
+    all_sent(sml_s.at[3], px.at[0:nz - 1])
     value = px[0]
     for i in range(1, nz):
         value = value + px[i]
@@ -574,21 +593,20 @@
     tfin[pl.ds(own, 1)] = value[None]
     copies = []
     for i, (ox, oy, ok) in enumerate(hall[1:]):
-        copies.append(remote(qtile, tfin.at[own], pz_s.at[i], pz_r.at[2, i], at_hall(ox, oy, ok)))
+        copies.append(remote(qtile, tfin.at[own], sml_s.at[4], sml_r.at[4], at_hall(ox, oy, ok)))
         copies[-1].start()
 
-    @pl.when(holds)
+    @pl.when(holds & (x == px_t))
     def _():
-        for copy in dia_row:
-            copy.wait_send()
-        for copy in dia_col[1:]:
-            copy.wait_send()
+        all_sent(dia_s.at[0], gcol.at[0:8 * (count + len(line) - 2), :])
 
     @pl.when(holds & (x != px_t))
     def _():
-        dia_col[0].wait_send()
-
-    wait_all(copies, "small4")
+        all_sent(dia_s.at[0], gcol.at[0:8 * (count + len(line) - 1), :])
+
+    with jax.named_scope("small4"):
+        all_here(sml_r.at[4], tfin.at[0:nk * count - 1])
+    all_sent(sml_s.at[4], tfin.at[0:nk * count - 1])
     trial = jnp.zeros((nx, BLK), jnp.float32)
     for h in range(nk):
         value = jnp.zeros((nx, BLK), jnp.float32)
@@ -629,7 +647,6 @@
     line = pltpu.VMEM((1, BLK), f32)
     lines = pltpu.VMEM((count, 1, BLK), f32)
     dma = pltpu.SemaphoreType.DMA
-    n_plane, n_line = count - 1, nz * nk
     grad, direction, trial, stat = pl.pallas_call(
         functools.partial(kernel, dims),
         out_shape=(
@@ -644,18 +661,18 @@
             pltpu.SMEM(bvec_index.shape, jnp.int32), pltpu.SMEM(weight_table.shape, f32),
             pltpu.VMEM(m_matrices.shape[1:], f32), pltpu.VMEM((rows, cols), f32), pltpu.VMEM((rows, cols), f32), dma((5,)),
             pltpu.VMEM((nx, 2, BLK, BLK), f32), block, pltpu.VMEM((nx, 8, BLK), f32), tile,
-            block, block, block, block, block, block, block, line, lines, lines,
+            block, block, block, block, block, block, block, block, line, lines, lines,
             wide, tall, wide, tall, tall, wide, tall, wide, wide, tall, wide, wide,
             pltpu.VMEM((2 * nx * BLK, 3 * BLK), jnp.bfloat16), pltpu.VMEM((count // 4, 2 * nx * BLK, 4 * BLK), f32),
             pltpu.VMEM((nk * count, nx, BLK), f32), pltpu.VMEM((nk * count, nx, BLK), f32), pltpu.VMEM((nz, nx, BLK), f32),
             half_tile, half_tile,
-            dma((nx - 1,)), dma((nx - 1,)),
-            dma((n_plane + n_line,)), dma((2 * nx,)),
-            dma((4,)), dma((4,)),
-            dma((2, 24)), dma((5, 24)),
-            dma((2, 8)), dma((5, 8)),
-            dma((2, nz)), dma((5, nz)),
-            dma((n_plane,)), dma((2, n_plane)), dma((nk * count,)), dma((3, nk * count)),
+            dma((1,)), dma((1,)),
+            dma((1,)), dma((2 * nx,)),
+            dma((1,)), dma((4,)),
+            dma((3,)), dma((3, 10)),
+            dma((3,)), dma((3, 9)),
+            dma((3,)), dma((3, 2)),
+            dma((5,)), dma((5,)),
         ],
         compiler_params=pltpu.CompilerParams(
             collective_id=0, has_side_effects=True, vmem_limit_bytes=40 * 1024 * 1024

time: 96.8 us -> 90.5 us (0.935)
  Pallas kernels: 96 us -> 89.8 us
    pallas_call x1, Pallas kernels: 95.2 us -> 89 us  [shards(): pl.pallas_call(functools.partial(kernel, dims), out_shape=(jax.ShapeDtype...]
where the time goes in v5:
time: 90.5 us; the launch traced here: 90.4 us
  Pallas kernels  89.8 us (99%)
    pallas_call x1, Pallas kernels, shards(): pl.pallas_call(functools.partial(kernel, dims), out_shape=(jax.ShapeDtype...  89 us

profile of v5, /device:TPU:1, one launch (start us, length us, event | category | flops | bytes accessed | tf_op | source)
XLA Modules:
  0.0 90.4 jit_solution(7515233228553044613)
XLA Ops:
  0.6 89.0 %shard_map.92 = (f32[128,512]{1,0:T(8,128)S(1)}, f32[128,512]{1,0:T(8,128)S(1)}, f32[32,4,128]{2,1,0:T(4,128)S(1)}, f32[8,128]{1,0:T(8,128)S(1)}) custom-call(f32[2,128,512]{2,1,0:T(8,128)} %bitcast.3, f32[128,512]{1,0:T(8,128)} %dp_in.1, f32[128,512]{1,0:T(8,128)} %gp_in.1, s32[4]{0:T(128)} %idx_in.1, f32[6]{0:T(128)} %tab_in.1), custom_call_target="tpu_custom_call" | custom-call | tf_op jit(solution)/shard_map/pallas_call | solution.py:650
  89.6 0.8 shard_map.93

commit v6 on v5

--- a/solution.py
+++ b/solution.py
@@ -204,13 +204,13 @@
             for i in range(3):
                 first[2 * i].wait_recv()
                 held = dst.at[top, lanes(nx * y + off(x, nx - ring_x[i], nx))]
-                for j in range(3):
+                for j in (2, 0, 1):
                     sem = group_sem(bank, ring_x[i], ring_y[j])
                     second.append(remote(held, held, row_s.at[bank], sem, at_plane(0, ring_y[j])))
                     second[-1].start()
                 first[2 * i + 1].wait_recv()
                 held = dst.at[low, lanes(nx * off(y, ny - ring_y[i], ny) + x)]
-                for j in range(3):
+                for j in (2, 0, 1):
                     sem = group_sem(bank, ring_x[j], ring_y[i])
                     second.append(remote(held, held, row_s.at[bank], sem, at_plane(ring_x[j], 0)))
                     second[-1].start()
@@ -224,7 +224,7 @@
 
     def plane_sum(state, left, right, acc, before_last=lambda: None):
         for pieces in groups:
-            if pieces is groups[-1]:
+            if pieces is groups[-2]:
                 before_last()
             places = plane_pieces(state, pieces)
             rows_l = jnp.concatenate([left[:, at] for at in places], axis=1)
@@ -502,13 +502,19 @@
     line_forward(cols)
     line_near(cols)
     plane_forward(rows)
-    line_finish(cols)
+    line_far(cols)
     plane_finish(more)
-
-    odd = jnp.zeros((BLK, BLK), jnp.float32)
-    for at in range(0, order, chunk):
-        right = gcol[at:at + chunk, :] + col4[at:at + chunk, :] * (1.0 / 5040.0)
-        odd = odd + dot_split(split(row3[:, at:at + chunk]), split(right))
+    line_mid(cols)
+
+    def odd_sum(acc, steps):
+        for at in part_of_sum(steps):
+            right = gcol[at, :] + col4[at, :] * (1.0 / 5040.0)
+            acc = acc + dot_split(split(row3[:, at]), split(right))
+        return acc
+
+    odd = odd_sum(jnp.zeros((BLK, BLK), jnp.float32), close)
+    line_done(cols)
+    odd = odd_sum(odd, distant)
     odd = odd + blk1[...] + blk3[...] * (1.0 / 6.0)
     def even_columns(at):
         return acol[at, :] + col4[at, :] * (1.0 / 40320.0)
@@ -532,13 +538,15 @@
         high, tail = split(jnp.concatenate([erow[:, at] for at in slots], axis=1))
         turned[g] = dot(mt[...], jnp.concatenate([high, high, tail], axis=0))
 
-    for g in range(len(groups) - 1):
+    for g in range(len(groups) - 2):
         turn(g)
     line_far(cols)
-    turn(len(groups) - 1)
+    for g in range(len(groups) - 2, len(groups)):
+        turn(g)
     plane_done(rows)
 
     hall = [(ox, oy, ok) for ox in range(nx) for oy in range(ny) for ok in range(nk)]
+    hall.sort(key=lambda step: min(step[0], nx - step[0]) + min(step[1], ny - step[1]))
 
     def at_hall(ox, oy, ok):
         return dev(off(x, ox, nx), off(y, oy, ny), z, off(k, ok, nk))
@@ -547,7 +555,7 @@
     line_done(cols)
     own = nk * c + k
     copies = []
-    for g, pieces in enumerate(groups):
+    for g, pieces in reversed(list(enumerate(groups))):
         for i, (ox, oy) in enumerate(pieces):
             back = (nx - ox) % nx, (ny - oy) % ny
             place = nx * off(y, back[1], ny) + off(x, back[0], nx)
@@ -580,7 +588,7 @@
     ttile[...] = value
     px[pl.ds(z, 1)] = value[None]
     copies = []
-    for oz in range(1, nz):
+    for oz in sorted(range(1, nz), key=lambda oz: -min(oz, nz - oz)):
         copies.append(remote(ttile, px.at[z], sml_s.at[3], sml_r.at[3], at_line(oz, 0)))
         copies[-1].start()
     with jax.named_scope("small3"):
@@ -592,7 +600,7 @@
     qtile[...] = value
     tfin[pl.ds(own, 1)] = value[None]
     copies = []
-    for i, (ox, oy, ok) in enumerate(hall[1:]):
+    for ox, oy, ok in reversed(hall[1:]):
         copies.append(remote(qtile, tfin.at[own], sml_s.at[4], sml_r.at[4], at_hall(ox, oy, ok)))
         copies[-1].start()
 

time: 90.5 us -> 88.2 us (0.975)
  Pallas kernels: 89.8 us -> 87.4 us
    pallas_call x1, Pallas kernels: 89 us -> 86.6 us  [shards(): pl.pallas_call(functools.partial(kernel, dims), out_shape=(jax.ShapeDtype...]
where the time goes in v6:
time: 88.2 us; the launch traced here: 88.1 us
  Pallas kernels  87.4 us (99%)
    pallas_call x1, Pallas kernels, shards(): pl.pallas_call(functools.partial(kernel, dims), out_shape=(jax.ShapeDtype...  86.6 us

profile of v6, /device:TPU:1, one launch (start us, length us, event | category | flops | bytes accessed | tf_op | source)
XLA Modules:
  0.0 88.1 jit_solution(17609832841332713251)
XLA Ops:
  0.6 86.6 %shard_map.92 = (f32[128,512]{1,0:T(8,128)S(1)}, f32[128,512]{1,0:T(8,128)S(1)}, f32[32,4,128]{2,1,0:T(4,128)S(1)}, f32[8,128]{1,0:T(8,128)S(1)}) custom-call(f32[2,128,512]{2,1,0:T(8,128)} %bitcast.3, f32[128,512]{1,0:T(8,128)} %dp_in.1, f32[128,512]{1,0:T(8,128)} %gp_in.1, s32[4]{0:T(128)} %idx_in.1, f32[6]{0:T(128)} %tab_in.1), custom_call_target="tpu_custom_call" | custom-call | tf_op jit(solution)/shard_map/pallas_call | solution.py:658
  87.2 0.8 shard_map.93

commit v7 on v6

--- a/solution.py
+++ b/solution.py
@@ -408,10 +408,10 @@
         return value
 
     copies = small_line(0, lambda index: stile, sx)
+    cols = line_start(1, gblk, column_slots(gcol))
+    rows = plane_start(0, gblk, grow)
     grow[:, lanes(c)] = total
     gcol[lanes(r), :] = total
-    rows = plane_start(0, gblk, grow)
-    cols = line_start(1, gblk, column_slots(gcol))
     with jax.named_scope("small0"):
         all_here(sml_r.at[0], sx.at[0:count - 1])
     all_sent(sml_s.at[0], sx.at[0:count - 1])
@@ -441,12 +441,11 @@
 
     chunk = 4 * BLK if order % (4 * BLK) == 0 else BLK
     beta_w = jnp.concatenate([beta] * nk, axis=1)
-    scale_w = jnp.concatenate([scale] * nk, axis=1)
 
     def square(acc, steps):
         for at in part_of_sum(steps):
-            left = scale_w * (beta_w * drow[:, at] - grow[:, at])
-            right = scale * (beta * dcol[at, :] - gcol[at, :])
+            left = beta_w * drow[:, at] - grow[:, at]
+            right = beta * dcol[at, :] - gcol[at, :]
             acol[at, :] = right
             acc = acc + dot_split(split(left), split(right))
         return acc
@@ -454,12 +453,13 @@
     acc = square(jnp.zeros((BLK, BLK), jnp.float32), close)
     line_done(cols)
     acc = square(acc, distant)
-    blk1[...] = acol[lanes(r), :]
+    acc = acc * scale * scale
+    blk1[...] = scale * acol[lanes(r), :]
     blk2[...] = acc
+    cols = line_start(2, blk2, column_slots(col2))
+    rows = plane_start(1, blk2, row2)
     row2[:, lanes(c)] = acc
     col2[lanes(r), :] = acc
-    rows = plane_start(1, blk2, row2)
-    cols = line_start(2, blk2, column_slots(col2))
     for j in range(nx):
         at = pl.ds(pl.multiple_of(y * wide + j * BLK, BLK), BLK)
         piece = grow[:, at]
@@ -477,6 +477,7 @@
     acc3 = plane_sum(
         rows, row2, lambda at: acol[at, :], jnp.zeros((BLK, BLK), jnp.float32), lambda: line_far(cols)
     )
+    acc3 = acc3 * scale
     blk3[...] = acc3
     row3[:, lanes(c)] = acc3
     more = plane_start(4, blk3, row3)
@@ -491,17 +492,17 @@
     line_done(cols)
     acc4 = fourth(acc4, distant)
     blk4[...] = acc4
+    cols = line_start(3, blk4, column_slots(col4))
+    rows = plane_start(2, blk4, row4)
     row4[:, lanes(c)] = acc4
     col4[lanes(r), :] = acc4
-    cols = line_start(3, blk4, column_slots(col4))
-    rows = plane_start(2, blk4, row4)
     plane_forward(more)
     for at in range(0, order, chunk):
         acol[at:at + chunk, :] = col2[at:at + chunk, :] * (1.0 / 720.0)
         gcol[at:at + chunk, :] = col2[at:at + chunk, :] * (1.0 / 120.0)
     line_forward(cols)
+    plane_forward(rows)
     line_near(cols)
-    plane_forward(rows)
     line_far(cols)
     plane_finish(more)
     line_mid(cols)

time: 88.2 us -> 88.1 us (level)
  no operation moved by 1% of the time
where the time goes in v7:
time: 88.1 us; the launch traced here: 87.9 us
  Pallas kernels  87.3 us (99%)
    pallas_call x1, Pallas kernels, shards(): pl.pallas_call(functools.partial(kernel, dims), out_shape=(jax.ShapeDtype...  86.5 us

profile of v7, /device:TPU:1, one launch (start us, length us, event | category | flops | bytes accessed | tf_op | source)
XLA Modules:
  0.0 87.9 jit_solution(7584847738031259683)
XLA Ops:
  0.6 86.5 %shard_map.92 = (f32[128,512]{1,0:T(8,128)S(1)}, f32[128,512]{1,0:T(8,128)S(1)}, f32[32,4,128]{2,1,0:T(4,128)S(1)}, f32[8,128]{1,0:T(8,128)S(1)}) custom-call(f32[2,128,512]{2,1,0:T(8,128)} %bitcast.3, f32[128,512]{1,0:T(8,128)} %dp_in.1, f32[128,512]{1,0:T(8,128)} %gp_in.1, s32[4]{0:T(128)} %idx_in.1, f32[6]{0:T(128)} %tab_in.1), custom_call_target="tpu_custom_call" | custom-call | tf_op jit(solution)/shard_map/pallas_call | solution.py:659
  87.1 0.8 shard_map.93
